TPU v7x, 128 devices: a whole 4x4x4 slice. The times are simulated.
128 devices in a mesh: grp: 8 (over x_lo, z), loc: 16 (over y, x_hi, core).
Axes of the slice: x: 4 (x_hi: 2, x_lo: 2; x = x_hi * 2 + x_lo), y: 4, z: 4, core: 2. Of those that a mesh axis runs over, the one named last changes fastest.
Arguments:
- features: float32 [131072, 256], P(('grp', 'loc')), may hold values from -6 to 6
- hub_block: bfloat16 [512, 131072], P(None, ('grp', 'loc')), may hold values from -0.0625 to 0.0625
- hub_slot: int32 [512], P(('grp', 'loc')), may hold values from 0 to 1023, as said below
- neighbours: int32 [131072, 16], P(('grp', 'loc')), may hold values from 0 to 3071
- counts: int32 [131072], P(('grp', 'loc')), may hold values from 1 to 16
- halo_send: int32 [2048, 128], P(('grp', 'loc')), may hold values from 0 to 1023
- weight: float32 [256, 256], replicated, may hold values from -0.375 to 0.375
- bias: float32 [256], replicated, may hold values from -3 to 3
Outputs:
- layer_out: float32 [131072, 256], P(('grp', 'loc'))
Inputs may be any that keep to these rules, and one draw needn't show every extreme that they name: `hub_slot`: within each aligned block of 4 entries the values are distinct.
All inputs are finite; a program needn't handle non-finite values.
Results may differ from a plain program's by a relative error of at most 0.0003.
Values sent between devices are 32-bit elements; how exact they have to be, the bound alone decides.
A program may use at most 64 MiB of HBM per device.

v0:
```python
import jax
import jax.numpy as jnp
from jax import lax
from jax.sharding import PartitionSpec as P


def cut_along(value, dim, length):
    dims = value.shape
    parts = value.reshape(*dims[:dim], length, dims[dim] // length, *dims[dim + 1 :])
    return jnp.moveaxis(parts, dim, 0)


def summed_on_arrival(value, axis, dim):
    length = lax.axis_size(axis)
    parts = lax.all_to_all(cut_along(value, dim, length), axis, 0, 0, tiled=True)
    return jnp.sum(parts, axis=0)


def on_device(features, hub_block, hub_slot, neighbours, counts, halo_send, weight, bias):
    width = features.shape[1]
    own_rows = features.shape[0]
    slot_total = neighbours.shape[1]
    rounded = features.astype(jnp.bfloat16)
    group_part = summed_on_arrival(
        jnp.dot(hub_block, rounded, preferred_element_type=jnp.float32), "grp", 0
    )
    hub_part = summed_on_arrival(group_part, "loc", 0)
    outgoing = features[halo_send.reshape(-1)]
    outgoing = outgoing.reshape(halo_send.shape[0], halo_send.shape[1], width)
    received = lax.all_to_all(outgoing, "loc", split_axis=0, concat_axis=0, tiled=True)
    pooled = jnp.concatenate([features, received.reshape(-1, width)], axis=0)
    pool_rows = pooled.shape[0]
    block_rows = 512
    block_count = own_rows // block_rows
    pool_index = jnp.arange(pool_rows, dtype=jnp.int32)

    def block_sum(pair):
        slots, used_counts = pair
        adjacency = jnp.zeros((slots.shape[0], pool_rows), jnp.float32)
        for slot_number in range(slot_total):
            active = (slot_number < used_counts)[:, None]
            hits = (slots[:, slot_number][:, None] == pool_index[None, :]) & active
            adjacency = adjacency + hits.astype(jnp.float32)
        summed = jnp.dot(
            adjacency, pooled, precision=lax.Precision.HIGHEST, preferred_element_type=jnp.float32
        )
        return summed / used_counts.astype(jnp.float32)[:, None]

    low = lax.map(
        block_sum,
        (
            neighbours.reshape(block_count, block_rows, slot_total),
            counts.reshape(block_count, block_rows),
        ),
    )
    low = low.reshape(own_rows, width)
    own_index = jnp.arange(own_rows, dtype=jnp.int32)
    hub_place = (own_index[:, None] == hub_slot[None, :]).astype(jnp.float32)
    hub_rows = jnp.dot(
        hub_place, hub_part, precision=lax.Precision.HIGHEST, preferred_element_type=jnp.float32
    )
    combined = features + low + hub_rows
    result = (
        jnp.dot(
            combined, weight, precision=lax.Precision.HIGHEST, preferred_element_type=jnp.float32
        )
        + bias
    )
    return jnp.maximum(result, 0.0)


def solution(mesh):
    in_specs = (
        P(("grp", "loc"), None),
        P(None, ("grp", "loc")),
        P(("grp", "loc")),
        P(("grp", "loc"), None),
        P(("grp", "loc")),
        P(("grp", "loc"), None),
        P(),
        P(),
    )
    out_specs = P(("grp", "loc"), None)
    return jax.shard_map(
        on_device, mesh=mesh, in_specs=in_specs, out_specs=out_specs, check_vma=False
    )
```

profile of v0, /device:TPU:1, one launch (start us, length us, event | category | flops | bytes accessed | tf_op | source)
XLA Modules:
  0.0 135.1 jit_solution(571897453638191810)
XLA Ops:
  0.0 1.2 copy-done
  1.2 2.5 %fusion.108 = f32[512,256]{1,0:T(8,128)} fusion(bf16[512,1024]{1,0:T(8,128)(2,1)S(1)} %copy-done, f32[1024,256]{1,0:T(8,128)} %param.10), kind=kOutput, calls=%fused_computation.125 | convolution fusion | flops 268697600 | bytes 2621440 | tf_op jit(solution)/shard_map/dot_general | solution.py:25
  3.7 6.8 %all-to-all-start.1 = ((f32[8,64,256]{2,1,0:T(8,128)}), f32[8,64,256]{2,1,0:T(8,128)S(1)}, u32[]{:S(2)}, u32[]{:S(2)}) async-start(f32[8,64,256]{2,1,0:T(8,128)} %bitcast.5), calls=%async_computation.1 | async-start | bytes 1048576 | tf_op jit(solution)/shard_map/all_to_all | solution.py:15
  10.5 7.7 %all-to-all-done.1 = f32[8,64,256]{2,1,0:T(8,128)S(1)} async-done(((f32[8,64,256]{2,1,0:T(8,128)}), f32[8,64,256]{2,1,0:T(8,128)S(1)}, u32[]{:S(2)}, u32[]{:S(2)}) %all-to-all-start.1) | async-done | bytes 524320 | tf_op jit(solution)/shard_map/all_to_all | solution.py:15
  18.3 0.7 reshape.180
  18.9 9.4 %all-to-all-start.2 = ((f32[16,4,256]{2,1,0:T(4,128)}), f32[16,4,256]{2,1,0:T(4,128)S(1)}, u32[]{:S(2)}, u32[]{:S(2)}) async-start(f32[16,4,256]{2,1,0:T(4,128)} %reshape.180), calls=%async_computation.2 | async-start | bytes 131072 | tf_op jit(solution)/shard_map/all_to_all | solution.py:15
  28.3 8.6 %gather_fusion = f32[2048,256]{1,0:T(8,128)} fusion(f32[1024,256]{1,0:T(8,128)S(1)} %copy-done.1, s32[2048]{0:T(1024)S(1)} %broadcast_clamp_fusion), kind=kCustom, calls=%fused_computation | custom fusion | bytes 4202496 | tf_op jit(solution)/shard_map/gather | solution.py:28
  36.9 0.0 all-to-all-done.2
  36.9 7.4 %all-to-all-start = ((f32[16,128,256]{2,1,0:T(8,128)}), f32[16,128,256]{2,1,0:T(8,128)}, u32[]{:S(2)}, u32[]{:S(2)}) async-start(f32[16,128,256]{2,1,0:T(8,128)} %bitcast.78), calls=%async_computation | async-start | bytes 4194304 | tf_op jit(solution)/shard_map/all_to_all | solution.py:30
  44.3 0.1 reshape.173
  44.4 28.3 %all-to-all-done = f32[16,128,256]{2,1,0:T(8,128)} async-done(((f32[16,128,256]{2,1,0:T(8,128)}), f32[16,128,256]{2,1,0:T(8,128)}, u32[]{:S(2)}, u32[]{:S(2)}) %all-to-all-start) | async-done | bytes 2097184 | tf_op jit(solution)/shard_map/all_to_all | solution.py:30
  72.7 3.5 %pad_maximum_fusion = f32[3072,256]{1,0:T(8,128)} fusion(f32[2048,256]{1,0:T(8,128)} %bitcast.3, f32[1024,256]{1,0:T(8,128)S(1)} %copy-done.1), kind=kLoop, calls=%fused_computation.120 | loop fusion | flops 786432 | bytes 6291456 | tf_op jit(solution)/shard_map/concatenate | solution.py:31
  76.2 55.7 %while.12 = (s32[]{:T(128)}, f32[2,512,256]{2,1,0:T(8,128)S(1)}, s32[2,512,16]{1,0,2:T(2,128)S(1)}, s32[2,512]{1,0:T(2,128)S(1)}, f32[3072,256]{1,0:T(8,128)}, /*index=5*/s32[]{:T(128)}) while((s32[]{:T(128)}, f32[2,512,256]{2,1,0:T(8,128)S(1)}, s32[2,512,16]{1,0,2:T(2,128)S(1)}, s32[2,512]{1,0:T(2,128)S(1)}, ...), condition=%wide.region_1.0_spmd.clone.clone, body=%wide.region_0.0_spmd.clone.clone.sunk | while | flops 4931068416 | bytes 3926097 | solution.py:49
  76.2 0.1 compare_reduce_fusion.17
  76.4 27.6 %fusion.127 = f32[2,512,256]{2,1,0:T(8,128)S(1)} fusion(f32[2,512,256]{2,1,0:T(8,128)S(1)} %get-tuple-element.290, s32[]{:T(128)} %get-tuple-element.289, f32[3072,256]{1,0:T(8,128)} %get-tuple-element.299, s32[512]{0:T(512)S(1)} %bitcast.81, s32[512]{0:T(512)S(1)} %bitcast.82, s32[512]{0:T(512)S(1)} %bitcast.83, s32[512]{0:T(512)S(1)} %bitcast.84, ...), kind=kOutput, calls=%fused_computation.100.clone.1 | convolution fusion | flops 4931059712 | bytes 3713028 | tf_op jit(solution)/shard_map/while/body/eval_jaxpr/dot_general | solution.py:44
  104.1 0.1 compare_reduce_fusion.17
  104.3 27.6 %fusion.127 = f32[2,512,256]{2,1,0:T(8,128)S(1)} fusion(f32[2,512,256]{2,1,0:T(8,128)S(1)} %get-tuple-element.290, s32[]{:T(128)} %get-tuple-element.289, f32[3072,256]{1,0:T(8,128)} %get-tuple-element.299, s32[512]{0:T(512)S(1)} %bitcast.81, s32[512]{0:T(512)S(1)} %bitcast.82, s32[512]{0:T(512)S(1)} %bitcast.83, s32[512]{0:T(512)S(1)} %bitcast.84, ...), kind=kOutput, calls=%fused_computation.100.clone.1 | convolution fusion | flops 4931059712 | bytes 3713028 | tf_op jit(solution)/shard_map/while/body/eval_jaxpr/dot_general | solution.py:44
  131.9 0.0 copy-start.7
  131.9 0.0 copy-start.2
  132.0 0.0 copy-start.6
  132.0 0.1 bitcast_add_fusion
  132.1 0.5 copy-done.7
  132.6 0.5 convolution_add_fusion
  133.2 2.0 %fusion.107 = f32[1024,256]{1,0:T(8,128)} fusion(f32[1024,256]{1,0:T(8,128)S(1)} %convolution_add_fusion, f32[256,256]{1,0:T(8,128)S(1)} %copy-done.2, f32[256]{0:T(256)S(1)} %copy-done.6), kind=kOutput, calls=%fused_computation.123 | convolution fusion | flops 805830656 | bytes 2360320 | tf_op jit(solution)/shard_map/dot_general | solution.py:64
  (25 shorter events, 0.3 us)
Async XLA Ops:
  0.0 1.2 copy-start
  0.0 28.3 %copy-start.1 = (f32[1024,256]{1,0:T(8,128)S(1)}, f32[1024,256]{1,0:T(8,128)}, u32[]{:S(2)}) copy-start(f32[1024,256]{1,0:T(8,128)} %param.10) | copy-start | bytes 3145732
  0.0 10.5 %copy-start.4 = (s32[16,128]{1,0:T(8,128)S(1)}, s32[16,128]{1,0:T(8,128)}, u32[]{:S(2)}) copy-start(s32[16,128]{1,0:T(8,128)} %param.15) | copy-start | bytes 24580
  3.7 14.5 %all-to-all-start.1 = ((f32[8,64,256]{2,1,0:T(8,128)}), f32[8,64,256]{2,1,0:T(8,128)S(1)}, u32[]{:S(2)}, u32[]{:S(2)}) async-start(f32[8,64,256]{2,1,0:T(8,128)} %bitcast.5), calls=%async_computation.1 | async-start | bytes 1048576 | tf_op jit(solution)/shard_map/all_to_all | solution.py:15
  18.9 18.0 %all-to-all-start.2 = ((f32[16,4,256]{2,1,0:T(4,128)}), f32[16,4,256]{2,1,0:T(4,128)S(1)}, u32[]{:S(2)}, u32[]{:S(2)}) async-start(f32[16,4,256]{2,1,0:T(4,128)} %reshape.180), calls=%async_computation.2 | async-start | bytes 131072 | tf_op jit(solution)/shard_map/all_to_all | solution.py:15
  36.9 7.4 %copy-start.3 = (s32[1024,16]{0,1:T(8,128)S(1)}, s32[1024,16]{0,1:T(8,128)}, u32[]{:S(2)}) copy-start(s32[1024,16]{0,1:T(8,128)} %param.13) | copy-start | bytes 196612
  36.9 7.5 %copy-start.5 = (s32[1024]{0:T(1024)S(1)}, s32[1024]{0:T(1024)}, u32[]{:S(2)}) copy-start(s32[1024]{0:T(1024)} %param.14) | copy-start | bytes 12292
  36.9 35.8 %all-to-all-start = ((f32[16,128,256]{2,1,0:T(8,128)}), f32[16,128,256]{2,1,0:T(8,128)}, u32[]{:S(2)}, u32[]{:S(2)}) async-start(f32[16,128,256]{2,1,0:T(8,128)} %bitcast.78), calls=%async_computation | async-start | bytes 4194304 | tf_op jit(solution)/shard_map/all_to_all | solution.py:30
  131.9 0.7 copy-start.7
  131.9 1.2 copy-start.2
  132.0 1.2 copy-start.6
where the time goes:
time: 136 us; the launch traced here: 135 us
  matrix products  60.3 us (44%)
  waiting for transfers between devices  36 us (26%)
  starting transfers between devices  23.5 us (17%)
  local copies, waits for them, and re-layouts  11.2 us (8%)
  other arithmetic  3.89 us (3%)
    dot_general x2, matrix products, block_sum(): jnp.dot(adjacency, pooled, precision=lax.Precision.HIGHEST, preferred_ele...  55.3 us
    all_to_all x1, waiting for transfers between devices, on_device(): lax.all_to_all(outgoing, 'loc', split_axis=0, concat_axis=0, tiled=True)  28.3 us
    all_to_all x2, starting transfers between devices, summed_on_arrival(): lax.all_to_all(cut_along(value, dim, length), axis, 0, 0, tiled=True)  16.2 us
    gather x1, local copies, waits for them, and re-layouts, on_device(): outgoing = features[halo_send.reshape(-1)]  8.56 us
    all_to_all x2, waiting for transfers between devices, summed_on_arrival(): lax.all_to_all(cut_along(value, dim, length), axis, 0, 0, tiled=True)  7.73 us
    all_to_all x1, starting transfers between devices, on_device(): lax.all_to_all(outgoing, 'loc', split_axis=0, concat_axis=0, tiled=True)  7.37 us
    concatenate x1, other arithmetic, on_device(): pooled = jnp.concatenate([features, received.reshape(-1, width)], axis=0)  3.46 us
  transfers between devices with their start and end apart: 3, of which 2 were waited for; matrix products, arithmetic and copies ran while one was open for 6% of the time, Pallas kernels for 0%

commit v1 on v0

v1 whole, which is shorter than its diff:
```python
import jax
import jax.numpy as jnp
from jax import lax
from jax.experimental import pallas as pl
from jax.experimental.pallas import tpu as pltpu
from jax.sharding import PartitionSpec as P

MESH = pl.DeviceIdType.MESH
NY, NXH, NC, NXL, NZ = 4, 2, 2, 2, 4
ROWS, WIDTH, SLOTS, SENT = 1024, 256, 16, 128
HUBS, HUB_OWN = 512, 4
FIELD_ROWS, FIELDS, FIELD_BITS = 512, 6, 5
CHUNK = 256

SEND_ORDER = (
    (2, 1, 0), (1, 0, 0), (3, 0, 0), (0, 1, 0),
    (1, 1, 1), (3, 1, 1), (2, 0, 1), (0, 1, 1),
    (1, 1, 0), (3, 1, 0), (2, 0, 0), (2, 1, 1),
    (1, 0, 1), (3, 0, 1), (0, 0, 1), (0, 0, 0),
)
TAKE_ORDER = ((0, 0), (0, 1), (2, 0), (2, 1), (1, 1), (3, 1), (1, 0), (3, 0))


def split2(value):
    high = value.astype(jnp.bfloat16)
    low = (value - high.astype(jnp.float32)).astype(jnp.bfloat16)
    return high, low


def mm(left, right):
    return jnp.dot(left, right, preferred_element_type=jnp.float32)


def kernel(
    feat_hbm, hub_hbm, slot_hbm, nbr_hbm, cnt_hbm, halo_hbm, weight_hbm, bias_hbm,
    out_ref,
    feat, hub, slot, nbr, cnt, halo, weight, bias,
    fhi, flo, halo_rel, one_hot, stage, recv,
    part, part_in, pair_sum, z_in, z_sum, plane_in,
    marks, recip, adjacency, total, w_hi, w_lo,
    in_sem, halo_send, halo_recv, a_sem, b_send, b_recv, c_send, c_recv,
):
    g, l = lax.axis_index("grp"), lax.axis_index("loc")
    y, xh, c = l // 4, (l // 2) % 2, l % 2
    xl, z = g // 4, g % 4
    x = xh * 2 + xl

    def loc_of(dy, dx, dc):
        return ((y + dy) % NY) * 4 + ((xh + dx) % NXH) * 2 + (c + dc) % NC

    def plane_of(dx, dy):
        tx, ty = (x + dx) % 4, (y + dy) % NY
        return (tx % 2) * 4 + z, ty * 4 + (tx // 2) * 2 + c

    loads = []
    for number, (source, target) in enumerate((
        (feat_hbm, feat), (halo_hbm, halo), (hub_hbm, hub), (nbr_hbm, nbr),
        (cnt_hbm, cnt), (weight_hbm, weight), (bias_hbm, bias), (slot_hbm, slot),
    )):
        copy = pltpu.make_async_copy(source, target, in_sem.at[number])
        copy.start()
        loads.append(copy)

    barrier = pltpu.get_barrier_semaphore()
    greeted = 0
    for step in SEND_ORDER:
        if step != (0, 0, 0):
            pl.semaphore_signal(barrier, inc=1, device_id=(g, loc_of(*step)), device_id_type=MESH)
            greeted += 1
    for dz in range(1, NZ):
        pl.semaphore_signal(
            barrier, inc=1, device_id=(xl * 4 + (z + dz) % NZ, l), device_id_type=MESH
        )
        greeted += 1
    for dx in (1, 3):
        for dy in range(NY):
            pl.semaphore_signal(barrier, inc=1, device_id=plane_of(dx, dy), device_id_type=MESH)
            greeted += 1

    loads[1].wait()
    for number, step in enumerate(SEND_ORDER):
        halo_rel[number : number + 1, :] = halo[pl.ds(loc_of(*step), 1), :]
    columns = halo_rel[...].T
    loads[0].wait()
    for start in range(0, ROWS, 256):
        high, low = split2(feat[start : start + 256, :])
        fhi[start : start + 256, :] = high
        flo[start : start + 256, :] = low
    lane = lax.broadcasted_iota(jnp.int32, (SENT, ROWS), 1)
    halo_copies = {}
    for group in range(4):
        for inner in range(4):
            number = group * 4 + inner
            one_hot[inner * SENT : (inner + 1) * SENT, :] = jnp.where(
                lane == columns[:, number : number + 1], 1.0, 0.0
            ).astype(jnp.bfloat16)
        rows = mm(one_hot[...], fhi[...]) + mm(one_hot[...], flo[...])
        for inner in range(4):
            number = group * 4 + inner
            step = SEND_ORDER[number]
            block = rows[inner * SENT : (inner + 1) * SENT, :]
            place = step[0] * NXH + step[1]
            if step == (0, 0, 0):
                recv[place, pl.ds(c, 1)] = block[None]
            else:
                stage[number] = block
        if group == 0:
            pl.semaphore_wait(barrier, greeted)
        for inner in range(4):
            number = group * 4 + inner
            step = SEND_ORDER[number]
            if step != (0, 0, 0):
                copy = pltpu.make_async_remote_copy(
                    src_ref=stage.at[number],
                    dst_ref=recv.at[step[0] * NXH + step[1], c],
                    send_sem=halo_send.at[number],
                    recv_sem=halo_recv.at[number],
                    device_id=(g, loc_of(*step)),
                    device_id_type=MESH,
                )
                copy.start()
                halo_copies[step] = copy

    loads[2].wait()
    upper = lax.broadcasted_iota(jnp.int32, (128, 128), 0) % 8 < 4
    for start in range(0, HUBS, 128):
        rows = mm(hub[start : start + 128, :], fhi[...])
        left, right = rows[:, :128], rows[:, 128:]
        part[0, start : start + 128, :] = jnp.where(upper, left, pltpu.roll(right, 4, 0))
        part[1, start : start + 128, :] = jnp.where(upper, pltpu.roll(left, 124, 0), right)
    pair_copy = pltpu.make_async_remote_copy(
        src_ref=part.at[1 - c],
        dst_ref=part_in,
        send_sem=a_sem.at[0],
        recv_sem=a_sem.at[1],
        device_id=(g, loc_of(0, 0, 1)),
        device_id_type=MESH,
    )
    pair_copy.start()

    loads[3].wait()
    loads[4].wait()
    slots, used = nbr[...], cnt[...]
    active = lax.broadcasted_iota(jnp.int32, (SLOTS, ROWS), 0) < used
    place = slots & (FIELD_ROWS - 1)
    one = jnp.where(active, jnp.left_shift(1, (slots >> 9) * FIELD_BITS), 0)
    inverse = jnp.broadcast_to(1.0 / used.astype(jnp.float32), (8, ROWS))
    for start in range(0, ROWS, 128):
        rows = slice(start, start + 128)
        marks[0, rows, :] = place[:, rows].T
        marks[1, rows, :] = one[:, rows].T
        recip[rows, :] = inverse[:, rows].T

    pool_lane = lax.broadcasted_iota(jnp.int32, (32, FIELD_ROWS), 1)

    def build(block, carry):
        rows = pl.ds(pl.multiple_of(block * 32, 32), 32)
        row_place, row_one = marks[0, rows, :], marks[1, rows, :]
        packed = jnp.zeros((32, FIELD_ROWS), jnp.int32)
        for k in range(SLOTS):
            packed = packed + jnp.where(
                row_place[:, k : k + 1] == pool_lane, row_one[:, k : k + 1], 0
            )
        for field in range(FIELDS):
            number = (packed >> (field * FIELD_BITS)) & (2**FIELD_BITS - 1)
            number = number.astype(jnp.float32).astype(jnp.bfloat16)
            adjacency[2 * field, rows, :] = number[:, :CHUNK]
            adjacency[2 * field + 1, rows, :] = number[:, CHUNK:]
        return carry

    lax.fori_loop(0, 8, build, 0)

    pair_copy.wait_recv()
    own = pl.ds(c, 1)
    pair_sum[...] = (part[own][0] + part_in[...]).reshape(NXL, NZ, 64, 128)
    z_copies = []
    for dz in range(1, NZ):
        to = (z + dz) % NZ
        copy = pltpu.make_async_remote_copy(
            src_ref=pair_sum.at[:, to],
            dst_ref=z_in.at[dz - 1],
            send_sem=b_send.at[dz - 1],
            recv_sem=b_recv.at[dz - 1],
            device_id=(xl * 4 + to, l),
            device_id_type=MESH,
        )
        copy.start()
        z_copies.append(copy)

    lax.fori_loop(8, 24, build, 0)

    for copy in z_copies:
        copy.wait_recv()
    for half in range(NXL):
        value = pair_sum[half, pl.ds(z, 1)][0]
        for dz in range(NZ - 1):
            value = value + z_in[dz, half]
        z_sum[half] = value.reshape(8, 8, 128)
    plane_copies = []
    for dx in range(4):
        for dy in range(NY):
            if (dx, dy) == (0, 0):
                continue
            tx, ty = (x + dx) % 4, (y + dy) % NY
            copy = pltpu.make_async_remote_copy(
                src_ref=z_sum.at[tx % 2, ty * 2 + tx // 2],
                dst_ref=plane_in.at[dx * 4 + dy],
                send_sem=c_send.at[dx * 4 + dy],
                recv_sem=c_recv.at[dx * 4 + dy],
                device_id=plane_of(dx, dy),
                device_id_type=MESH,
            )
            copy.start()
            plane_copies.append(copy)

    lax.fori_loop(24, 32, build, 0)

    for number in range(4):
        rows = slice(number * CHUNK, (number + 1) * CHUNK)
        value = mm(adjacency[number], fhi[rows, :]) + mm(adjacency[number], flo[rows, :])
        total[...] = value if number == 0 else total[...] + value

    loads[5].wait()
    loads[6].wait()
    loads[7].wait()
    w_hi[...], w_lo[...] = split2(weight[...])

    for number, (dy, dx) in enumerate(TAKE_ORDER):
        for dc in range(NC):
            if (dy, dx, dc) != (0, 0, 0):
                halo_copies[(dy, dx, dc)].wait_recv()
        chip = ((y + NY - dy) % NY) * 2 + (xh + NXH - dx) % NXH
        high, low = split2(recv[dy * NXH + dx].reshape(CHUNK, WIDTH))
        links = adjacency[pl.ds(4 + chip, 1)][0]
        total[...] += mm(links, high) + mm(links, low)

    for copy in plane_copies:
        copy.wait_recv()
    hub_tile = z_sum[pl.ds(xl, 1), pl.ds(y * 2 + xh, 1)][0, 0]
    for number in range(1, 16):
        hub_tile = hub_tile + plane_in[number]
    for start in range(0, ROWS, 256):
        rows = slice(start, start + 256)
        index = lax.broadcasted_iota(jnp.int32, (256, WIDTH), 0) + start
        hub_add = jnp.zeros((256, WIDTH), jnp.float32)
        for r in range(HUB_OWN):
            row = jnp.concatenate([hub_tile[r : r + 1, :], hub_tile[4 + r : 5 + r, :]], axis=1)
            hub_add = jnp.where(index == slot[r], row, hub_add)
        combined = feat[rows, :] + total[rows, :] * recip[rows, 0:1] + hub_add
        high, low = split2(combined)
        value = mm(high, w_hi[...]) + mm(low, w_hi[...]) + mm(high, w_lo[...]) + bias[...]
        out_ref[rows, :] = jnp.maximum(value, 0.0)

    for copy in halo_copies.values():
        copy.wait_send()
    pair_copy.wait_send()
    for copy in z_copies + plane_copies:
        copy.wait_send()


def on_device(features, hub_block, hub_slot, neighbours, counts, halo_send, weight, bias):
    f32, bf16, i32 = jnp.float32, jnp.bfloat16, jnp.int32
    vmem, dma = pltpu.VMEM, pltpu.SemaphoreType.DMA
    return pl.pallas_call(
        kernel,
        out_shape=jax.ShapeDtypeStruct((ROWS, WIDTH), f32),
        in_specs=[pl.BlockSpec(memory_space=pltpu.HBM)] * 8,
        out_specs=pl.BlockSpec(memory_space=pltpu.VMEM),
        scratch_shapes=[
            vmem((ROWS, WIDTH), f32),
            vmem((HUBS, ROWS), bf16),
            pltpu.SMEM((HUB_OWN,), i32),
            vmem((SLOTS, ROWS), i32),
            vmem((1, ROWS), i32),
            vmem((16, SENT), i32),
            vmem((WIDTH, WIDTH), f32),
            vmem((1, WIDTH), f32),
            vmem((ROWS, WIDTH), bf16),
            vmem((ROWS, WIDTH), bf16),
            vmem((16, SENT), i32),
            vmem((4 * SENT, ROWS), bf16),
            vmem((16, SENT, WIDTH), f32),
            vmem((8, NC, SENT, WIDTH), f32),
            vmem((NC, HUBS, 128), f32),
            vmem((HUBS, 128), f32),
            vmem((NXL, NZ, 64, 128), f32),
            vmem((NZ - 1, NXL, 64, 128), f32),
            vmem((NXL, 8, 8, 128), f32),
            vmem((16, 8, 128), f32),
            vmem((2, ROWS, SLOTS), i32),
            vmem((ROWS, 8), f32),
            vmem((2 * FIELDS, ROWS, CHUNK), bf16),
            vmem((ROWS, WIDTH), f32),
            vmem((WIDTH, WIDTH), bf16),
            vmem((WIDTH, WIDTH), bf16),
            dma((8,)), dma((16,)), dma((16,)), dma((2,)),
            dma((3,)), dma((3,)), dma((16,)), dma((16,)),
        ],
        compiler_params=pltpu.CompilerParams(
            collective_id=0, has_side_effects=True, vmem_limit_bytes=40 * 1024 * 1024
        ),
    )(
        features, hub_block, hub_slot, neighbours.T, counts.reshape(1, -1), halo_send,
        weight, bias.reshape(1, -1),
    )


def solution(mesh):
    in_specs = (
        P(("grp", "loc"), None),
        P(None, ("grp", "loc")),
        P(("grp", "loc")),
        P(("grp", "loc"), None),
        P(("grp", "loc")),
        P(("grp", "loc"), None),
        P(),
        P(),
    )
    out_specs = P(("grp", "loc"), None)
    return jax.shard_map(
        on_device, mesh=mesh, in_specs=in_specs, out_specs=out_specs, check_vma=False
    )
```

time: 136 us -> 46 us (0.34)
  matrix products: 60.3 us -> 0 us
  Pallas kernels: 0 us -> 39.1 us
  waiting for transfers between devices: 36 us -> 0 us
  starting transfers between devices: 23.5 us -> 0 us
  local copies, waits for them, and re-layouts: 11.2 us -> 6.6 us
  other arithmetic: 3.89 us -> 0 us
    dot_general x5 -> x0, matrix products: 60.3 us -> none  [the longest x2 55.3 us: block_sum(): jnp.dot(adjacency, pooled, precision=lax.Precision.HIGHEST, preferred_ele...]
    pallas_call x0 -> x1, Pallas kernels: none -> 39.1 us  [on_device(): pl.pallas_call(kernel, out_shape=jax.ShapeDtypeStruct((ROWS, WIDTH), f32)...]
    all_to_all x3 -> x0, waiting for transfers between devices: 36 us -> none  [the longest x1 28.3 us: on_device(): lax.all_to_all(outgoing, 'loc', split_axis=0, concat_axis=0, tiled=True)]
    all_to_all x3 -> x0, starting transfers between devices: 23.5 us -> none  [the longest x2 16.2 us: summed_on_arrival(): lax.all_to_all(cut_along(value, dim, length), axis, 0, 0, tiled=True)]
    gather x1 -> x0, local copies, waits for them, and re-layouts: 8.56 us -> none  [on_device(): outgoing = features[halo_send.reshape(-1)]]
    unnamed x16 -> x17, local copies, waits for them, and re-layouts: 1.74 us -> 6.6 us
    concatenate x1 -> x0, other arithmetic: 3.46 us -> none  [on_device(): pooled = jnp.concatenate([features, received.reshape(-1, width)], axis=0)]
  transfers between devices with their start and end apart: 3 -> 0, of which waited for: 2 -> 0; matrix products, arithmetic and copies ran while one was open for 6% -> 0% of each run, Pallas kernels for 0% -> 0%
where the time goes in v1:
time: 46 us; the launch traced here: 45.7 us
  Pallas kernels  39.1 us (85%)
  local copies, waits for them, and re-layouts  6.6 us (14%)
    pallas_call x1, Pallas kernels, on_device(): pl.pallas_call(kernel, out_shape=jax.ShapeDtypeStruct((ROWS, WIDTH), f32)...  39.1 us
    unnamed x17, local copies, waits for them, and re-layouts  6.6 us

profile of v1, /device:TPU:1, one launch (start us, length us, event | category | flops | bytes accessed | tf_op | source)
XLA Modules:
  0.0 45.7 jit_solution(4869396849733450578)
XLA Ops:
  0.0 0.0 copy-start.5
  0.0 0.0 copy-start.6
  0.0 0.0 copy-start.7
  0.0 0.7 %copy-done.5 = s32[1024]{0:T(1024)S(1)} copy-done((s32[1024]{0:T(1024)S(1)}, s32[1024]{0:T(1024)}, u32[]{:S(2)}) %copy-start.5) | copy-done | bytes 4120
  0.7 0.0 copy-done.6
  0.7 0.0 copy-done.7
  0.7 0.0 copy-start
  0.7 1.2 %copy-done = f32[1024,256]{1,0:T(8,128)S(1)} copy-done((f32[1024,256]{1,0:T(8,128)S(1)}, f32[1024,256]{1,0:T(8,128)}, u32[]{:S(2)}) %copy-start) | copy-done | bytes 1048600
  1.9 0.0 copy-start.1
  1.9 1.2 %copy-done.1 = bf16[512,1024]{1,0:T(8,128)(2,1)S(1)} copy-done((bf16[512,1024]{1,0:T(8,128)(2,1)S(1)}, bf16[512,1024]{1,0:T(8,128)(2,1)}, u32[]{:S(2)}) %copy-start.1) | copy-done | bytes 1048600
  3.1 0.0 copy-start.2
  3.2 0.9 %copy-done.2 = f32[256,256]{1,0:T(8,128)S(1)} copy-done((f32[256,256]{1,0:T(8,128)S(1)}, f32[256,256]{1,0:T(8,128)}, u32[]{:S(2)}) %copy-start.2) | copy-done | bytes 262168
  4.1 0.0 copy-start.3
  4.1 0.8 %copy-done.3 = s32[1024,16]{0,1:T(8,128)S(1)} copy-done((s32[1024,16]{0,1:T(8,128)S(1)}, s32[1024,16]{0,1:T(8,128)}, u32[]{:S(2)}) %copy-start.3) | copy-done | bytes 65560
  4.9 0.0 copy-start.4
  4.9 0.7 %copy-done.4 = s32[16,128]{1,0:T(8,128)S(1)} copy-done((s32[16,128]{1,0:T(8,128)S(1)}, s32[16,128]{1,0:T(8,128)}, u32[]{:S(2)}) %copy-start.4) | copy-done | bytes 8216
  5.6 39.1 %shard_map.82 = f32[1024,256]{1,0:T(8,128)S(1)} custom-call(f32[1024,256]{1,0:T(8,128)S(1)} %copy-done, bf16[512,1024]{1,0:T(8,128)(2,1)S(1)} %copy-done.1, s32[4]{0:T(128)S(1)} %copy-done.7, s32[16,1024]{1,0:T(8,128)S(1)} %bitcast.3, s32[1,1024]{1,0:T(1,128)S(1)} %bitcast.4, s32[16,128]{1,0:T(8,128)S(1)} %copy-done.4, f32[256,256]{1,0:T(8,128)S(1)} %copy-done.2, ...), custom_call_target="tpu_custom_call" | custom-call | tf_op jit(solution)/shard_map/pallas_call | solution.py:264
  44.7 1.0 %copy.10 = f32[1024,256]{1,0:T(8,128)} copy(f32[1024,256]{1,0:T(8,128)S(1)} %shard_map.82) | data formatting | bytes 2097152
Async XLA Ops:
  0.0 0.7 %copy-start.5 = (s32[1024]{0:T(1024)S(1)}, s32[1024]{0:T(1024)}, u32[]{:S(2)}) copy-start(s32[1024]{0:T(1024)} %param.12) | copy-start | bytes 12292
  0.0 0.7 %copy-start.6 = (f32[256]{0:T(256)S(1)}, f32[256]{0:T(256)}, u32[]{:S(2)}) copy-start(f32[256]{0:T(256)} %param.15) | copy-start | bytes 3076
  0.0 0.7 %copy-start.7 = (s32[4]{0:T(128)S(1)}, s32[4]{0:T(128)}, u32[]{:S(2)}) copy-start(s32[4]{0:T(128)} %slot_hbm.1) | copy-start | bytes 52
  0.7 1.2 %copy-start = (f32[1024,256]{1,0:T(8,128)S(1)}, f32[1024,256]{1,0:T(8,128)}, u32[]{:S(2)}) copy-start(f32[1024,256]{1,0:T(8,128)} %feat_hbm.1) | copy-start | bytes 3145732
  1.9 1.2 %copy-start.1 = (bf16[512,1024]{1,0:T(8,128)(2,1)S(1)}, bf16[512,1024]{1,0:T(8,128)(2,1)}, u32[]{:S(2)}) copy-start(bf16[512,1024]{1,0:T(8,128)(2,1)} %hub_hbm.1) | copy-start | bytes 3145732
  3.1 0.9 %copy-start.2 = (f32[256,256]{1,0:T(8,128)S(1)}, f32[256,256]{1,0:T(8,128)}, u32[]{:S(2)}) copy-start(f32[256,256]{1,0:T(8,128)} %weight_hbm.1) | copy-start | bytes 786436
  4.1 0.8 %copy-start.3 = (s32[1024,16]{0,1:T(8,128)S(1)}, s32[1024,16]{0,1:T(8,128)}, u32[]{:S(2)}) copy-start(s32[1024,16]{0,1:T(8,128)} %param.11) | copy-start | bytes 196612
  4.9 0.7 %copy-start.4 = (s32[16,128]{1,0:T(8,128)S(1)}, s32[16,128]{1,0:T(8,128)}, u32[]{:S(2)}) copy-start(s32[16,128]{1,0:T(8,128)} %halo_hbm.1) | copy-start | bytes 24580

commit v2 on v1

--- a/solution.py
+++ b/solution.py
@@ -300,8 +300,13 @@
             collective_id=0, has_side_effects=True, vmem_limit_bytes=40 * 1024 * 1024
         ),
     )(
-        features, hub_block, hub_slot, neighbours.T, counts.reshape(1, -1), halo_send,
-        weight, bias.reshape(1, -1),
+        *(
+            pltpu.with_memory_space_constraint(array, pltpu.HBM)
+            for array in (
+                features, hub_block, hub_slot, neighbours.T, counts.reshape(1, -1), halo_send,
+                weight, bias.reshape(1, -1),
+            )
+        )
     )
 
 

time: 46 us -> 39.9 us (0.87)
  local copies, waits for them, and re-layouts: 6.6 us -> 0.97 us
    unnamed x17 -> x1, local copies, waits for them, and re-layouts: 6.6 us -> 0.97 us
where the time goes in v2:
time: 39.9 us; the launch traced here: 39.8 us
  Pallas kernels  38.8 us (97%)
  local copies, waits for them, and re-layouts  0.97 us (2%)
    pallas_call x1, Pallas kernels, on_device(): pl.pallas_call(kernel, out_shape=jax.ShapeDtypeStruct((ROWS, WIDTH), f32)...  38.8 us
    unnamed x1, local copies, waits for them, and re-layouts  0.97 us

profile of v2, /device:TPU:1, one launch (start us, length us, event | category | flops | bytes accessed | tf_op | source)
XLA Modules:
  0.0 39.8 jit_solution(11789059546793593085)
XLA Ops:
  0.0 38.8 %shard_map.82 = f32[1024,256]{1,0:T(8,128)S(1)} custom-call(f32[1024,256]{1,0:T(8,128)} %feat_hbm.1, bf16[512,1024]{1,0:T(8,128)(2,1)} %hub_hbm.1, s32[4]{0:T(128)} %slot_hbm.1, s32[16,1024]{1,0:T(8,128)} %bitcast.3, s32[1,1024]{1,0:T(1,128)} %bitcast.4, s32[16,128]{1,0:T(8,128)} %halo_hbm.1, f32[256,256]{1,0:T(8,128)} %weight_hbm.1, f32[1,256]{1,0:T(1,128)} %bitcast.5), custom_call_target="tpu_custom_call" | custom-call | tf_op jit(solution)/shard_map/pallas_call | solution.py:264
  38.8 1.0 %copy.10 = f32[1024,256]{1,0:T(8,128)} copy(f32[1024,256]{1,0:T(8,128)S(1)} %shard_map.82) | data formatting | bytes 2097152

commit v3 on v2

v3 whole, which is shorter than its diff:
```python
import jax
import jax.numpy as jnp
from jax import lax
from jax.experimental import pallas as pl
from jax.experimental.pallas import tpu as pltpu
from jax.sharding import PartitionSpec as P

MESH = pl.DeviceIdType.MESH
NY, NXH, NC, NXL, NZ = 4, 2, 2, 2, 4
ROWS, WIDTH, SLOTS, SENT = 1024, 256, 16, 128
HUBS, HUB_OWN = 512, 4
FIELD_ROWS, FIELDS, FIELD_BITS = 512, 6, 5

SEND_ORDER = (
    (2, 1, 0), (1, 0, 0), (2, 1, 1), (3, 0, 0),
    (1, 1, 0), (1, 1, 1), (2, 0, 0), (0, 0, 1),
    (3, 1, 0), (3, 1, 1), (2, 0, 1), (0, 0, 0),
    (0, 1, 0), (0, 1, 1), (1, 0, 1), (3, 0, 1),
)
GROUPS = (2, 2, 4, 4, 4)
TAKE_ORDER = (
    (0, 0, 0), (0, 0, 1), (2, 1, 0), (1, 0, 0), (3, 0, 0), (2, 1, 1), (1, 1, 0), (1, 1, 1),
    (2, 0, 0), (3, 1, 0), (3, 1, 1), (2, 0, 1), (1, 0, 1), (3, 0, 1), (0, 1, 0), (0, 1, 1),
)

def split2(value):
    high = value.astype(jnp.bfloat16)
    low = (value - high.astype(jnp.float32)).astype(jnp.bfloat16)
    return high, low


def mm(left, right):
    return jnp.dot(left, right, preferred_element_type=jnp.float32)


def scope(name):
    return jax.named_scope(name)


def kernel(
    feat_hbm, hub_hbm, slot_hbm, nbr_hbm, cnt_hbm, halo_hbm, weight_hbm, bias_hbm,
    out_ref,
    feat, hub, slot, nbr, cnt, halo, weight, bias,
    fhi, base, ghi, glo, halo_rel, one_hot, stage, recv,
    part, part_in, pair_sum, z_in, z_sum, plane_in,
    marks, recip, hub_mark, links_own, links_far, total, w_hi, w_lo,
    in_sem, halo_send, halo_recv, a_sem, b_send, b_recv, c_send, c_recv,
):
    g, l = lax.axis_index("grp"), lax.axis_index("loc")
    y, xh, c = l // 4, (l // 2) % 2, l % 2
    xl, z = g // 4, g % 4
    x = xh * 2 + xl

    def loc_of(dy, dx, dc):
        return ((y + dy) % NY) * 4 + ((xh + dx) % NXH) * 2 + (c + dc) % NC

    def plane_of(dx, dy):
        tx, ty = (x + dx) % 4, (y + dy) % NY
        return (tx % 2) * 4 + z, ty * 4 + (tx // 2) * 2 + c

    loads = []
    for number, (source, target) in enumerate((
        (feat_hbm, feat), (halo_hbm, halo), (weight_hbm, weight), (hub_hbm, hub), (nbr_hbm, nbr),
        (cnt_hbm, cnt), (bias_hbm, bias), (slot_hbm, slot),
    )):
        copy = pltpu.make_async_copy(source, target, in_sem.at[number])
        copy.start()
        loads.append(copy)

    with scope("greet"):
        barrier = pltpu.get_barrier_semaphore()
        greeted = 0
        for dx, dy in ((1, 2), (3, 2), (1, 1), (1, 3), (3, 1), (3, 3), (1, 0), (3, 0)):
            pl.semaphore_signal(barrier, inc=1, device_id=plane_of(dx, dy), device_id_type=MESH)
            greeted += 1
        for step in SEND_ORDER:
            if step != (0, 0, 0):
                pl.semaphore_signal(
                    barrier, inc=1, device_id=(g, loc_of(*step)), device_id_type=MESH
                )
                greeted += 1
        for dz in range(1, NZ):
            pl.semaphore_signal(
                barrier, inc=1, device_id=(xl * 4 + (z + dz) % NZ, l), device_id_type=MESH
            )
            greeted += 1

    with scope("halo_idx"):
        loads[1].wait()
        for number, step in enumerate(SEND_ORDER):
            halo_rel[number : number + 1, :] = halo[pl.ds(loc_of(*step), 1), :]
        columns = halo_rel[...].T
        loads[2].wait()
        w_hi[...], w_lo[...] = split2(weight[...])
        loads[0].wait()
    with scope("fw"):
        for start in range(0, ROWS, 256):
            rows = slice(start, start + 256)
            high, low = split2(feat[rows, :])
            fhi[rows, :] = high
            value = mm(high, w_hi[...]) + mm(low, w_hi[...]) + mm(high, w_lo[...])
            base[rows, :] = value
            ghi[rows, :], glo[rows, :] = split2(value)

    lane = lax.broadcasted_iota(jnp.int32, (SENT, ROWS), 1)
    halo_copies = {}

    def gather(group):
        first, size = sum(GROUPS[:group]), GROUPS[group]
        with scope(f"oh{group}"):
            for inner in range(size):
                number = first + inner
                one_hot[inner * SENT : (inner + 1) * SENT, :] = jnp.where(
                    lane == columns[:, number : number + 1], 1.0, 0.0
                ).astype(jnp.bfloat16)
        with scope(f"gmm{group}"):
            hot = one_hot[: size * SENT, :]
            rows = mm(hot, ghi[...]) + mm(hot, glo[...])
            for inner in range(size):
                number = first + inner
                block = rows[inner * SENT : (inner + 1) * SENT, :]
                if SEND_ORDER[number] == (0, 0, 0):
                    recv[number] = block
                else:
                    stage[number] = block

    def send(group):
        first, size = sum(GROUPS[:group]), GROUPS[group]
        for number in range(first, first + size):
            step = SEND_ORDER[number]
            if step != (0, 0, 0):
                copy = pltpu.make_async_remote_copy(
                    src_ref=stage.at[number],
                    dst_ref=recv.at[number],
                    send_sem=halo_send.at[number],
                    recv_sem=halo_recv.at[number],
                    device_id=(g, loc_of(*step)),
                    device_id_type=MESH,
                )
                copy.start()
                halo_copies[step] = copy

    gather(0)
    with scope("barrier"):
        pl.semaphore_wait(barrier, greeted)
    send(0)
    gather(1)
    send(1)

    with scope("hubpart"):
        loads[3].wait()
        upper = lax.broadcasted_iota(jnp.int32, (128, 128), 0) % 8 < 4
        for start in range(0, HUBS, 128):
            rows = mm(hub[start : start + 128, :], fhi[...])
            left, right = rows[:, :128], rows[:, 128:]
            part[0, start : start + 128, :] = jnp.where(upper, left, pltpu.roll(right, 4, 0))
            part[1, start : start + 128, :] = jnp.where(upper, pltpu.roll(left, 124, 0), right)
        pair_copy = pltpu.make_async_remote_copy(
            src_ref=part.at[1 - c],
            dst_ref=part_in,
            send_sem=a_sem.at[0],
            recv_sem=a_sem.at[1],
            device_id=(g, loc_of(0, 0, 1)),
            device_id_type=MESH,
        )
        pair_copy.start()

    gather(2)
    send(2)
    with scope("a_to_b"):
        pair_copy.wait_recv()
        pair_sum[...] = (part[pl.ds(c, 1)][0] + part_in[...]).reshape(NXL, NZ, 64, 128)
        z_copies = []
        for dz in range(1, NZ):
            to = (z + dz) % NZ
            copy = pltpu.make_async_remote_copy(
                src_ref=pair_sum.at[:, to],
                dst_ref=z_in.at[dz - 1],
                send_sem=b_send.at[dz - 1],
                recv_sem=b_recv.at[dz - 1],
                device_id=(xl * 4 + to, l),
                device_id_type=MESH,
            )
            copy.start()
            z_copies.append(copy)

    gather(3)
    gather(4)

    with scope("marks"):
        loads[4].wait()
        loads[5].wait()
        slots, used = nbr[...], cnt[...]
        active = lax.broadcasted_iota(jnp.int32, (SLOTS, ROWS), 0) < used
        place = slots & (FIELD_ROWS - 1)
        one = jnp.where(active, jnp.left_shift(1, (slots >> 9) * FIELD_BITS), 0)
        inverse = jnp.broadcast_to(1.0 / used.astype(jnp.float32), (8, ROWS))
        for start in range(0, ROWS, 128):
            rows = slice(start, start + 128)
            marks[0, rows, :] = place[:, rows].T
            marks[1, rows, :] = one[:, rows].T
            recip[rows, :] = inverse[:, rows].T

    pool_lane = lax.broadcasted_iota(jnp.int32, (32, FIELD_ROWS), 1)

    def build(block, carry):
        rows = pl.ds(pl.multiple_of(block * 32, 32), 32)
        row_place, row_one = marks[0, rows, :], marks[1, rows, :]
        packed = jnp.zeros((32, FIELD_ROWS), jnp.int32)
        for k in range(SLOTS):
            packed = packed + jnp.where(
                row_place[:, k : k + 1] == pool_lane, row_one[:, k : k + 1], 0
            )
        for field in range(FIELDS):
            number = (packed >> (field * FIELD_BITS)) & (2**FIELD_BITS - 1)
            number = number.astype(jnp.float32).astype(jnp.bfloat16)
            if field < 2:
                links_own[2 * field, rows, :] = number[:, :256]
                links_own[2 * field + 1, rows, :] = number[:, 256:]
            else:
                for peer in range(4):
                    links_far[(field - 2) * 4 + peer, rows, :] = number[
                        :, peer * SENT : (peer + 1) * SENT
                    ]
        return carry

    with scope("build1"):
        lax.fori_loop(0, 8, build, 0)

    with scope("b_to_c"):
        for copy in z_copies:
            copy.wait_recv()
        for half in range(NXL):
            value = pair_sum[half, pl.ds(z, 1)][0]
            for dz in range(NZ - 1):
                value = value + z_in[dz, half]
            z_sum[half] = value.reshape(8, 8, 128)
        plane_copies = []
        for dx in range(4):
            for dy in range(NY):
                if (dx, dy) == (0, 0):
                    continue
                tx, ty = (x + dx) % 4, (y + dy) % NY
                copy = pltpu.make_async_remote_copy(
                    src_ref=z_sum.at[tx % 2, ty * 2 + tx // 2],
                    dst_ref=plane_in.at[dx * 4 + dy],
                    send_sem=c_send.at[dx * 4 + dy],
                    recv_sem=c_recv.at[dx * 4 + dy],
                    device_id=plane_of(dx, dy),
                    device_id_type=MESH,
                )
                copy.start()
                plane_copies.append(copy)

    send(3)
    send(4)

    with scope("build3"):
        lax.fori_loop(8, 32, build, 0)

    with scope("hub_mark"):
        loads[6].wait()
        loads[7].wait()
        for r in range(HUB_OWN):
            hit = lax.broadcasted_iota(jnp.int32, (ROWS, WIDTH), 0) == slot[r]
            hub_mark[r] = jnp.where(hit, 1.0, 0.0)
        base[...] = base[...] + bias[...]

    with scope("own"):
        for number in range(4):
            rows = slice(number * 256, (number + 1) * 256)
            value = mm(links_own[number], ghi[rows, :]) + mm(links_own[number], glo[rows, :])
            total[...] = value if number == 0 else total[...] + value

    def far(step):
        number = SEND_ORDER.index(step)
        dy, dx, dc = step
        if step != (0, 0, 0):
            with scope(f"wait{dy}{dx}{dc}"):
                halo_copies[step].wait_recv()
        peer = loc_of(-dy, -dx, -dc)
        high, low = split2(recv[number])
        return peer, jnp.concatenate([high, low], axis=0)

    def linked(peer, rows):
        links = links_far[pl.ds(peer, 1), rows, :][0]
        return jnp.concatenate([links, links], axis=1)

    for number, step in enumerate(TAKE_ORDER[:-1]):
        peer, values = far(step)
        with scope(f"take{number}"):
            total[...] += mm(linked(peer, slice(None)), values)

    peer, values = far(TAKE_ORDER[-1])
    with scope("wait_c"):
        for copy in plane_copies:
            copy.wait_recv()
    with scope("hub_rows"):
        hub_tile = z_sum[pl.ds(xl, 1), pl.ds(y * 2 + xh, 1)][0, 0]
        for source in range(1, 16):
            hub_tile = hub_tile + plane_in[source]
        hub_own = jnp.concatenate([hub_tile, pltpu.roll(hub_tile, 4, 0)], axis=1)
        high, low = split2(hub_own)
        hub_own = mm(high, w_hi[...]) + mm(low, w_hi[...]) + mm(high, w_lo[...])
    with scope("final"):
        for start in range(0, ROWS, 256):
            rows = slice(start, start + 256)
            value = total[rows, :] + mm(linked(peer, rows), values)
            value = base[rows, :] + value * recip[rows, 0:1]
            for r in range(HUB_OWN):
                value = value + hub_mark[r, rows, :] * hub_own[r : r + 1, :]
            out_ref[rows, :] = jnp.maximum(value, 0.0)

    with scope("wait_send"):
        for copy in halo_copies.values():
            copy.wait_send()
        pair_copy.wait_send()
        for copy in z_copies + plane_copies:
            copy.wait_send()


def on_device(features, hub_block, hub_slot, neighbours, counts, halo_send, weight, bias):
    f32, bf16, i32 = jnp.float32, jnp.bfloat16, jnp.int32
    vmem, dma = pltpu.VMEM, pltpu.SemaphoreType.DMA
    return pl.pallas_call(
        kernel,
        out_shape=jax.ShapeDtypeStruct((ROWS, WIDTH), f32),
        in_specs=[pl.BlockSpec(memory_space=pltpu.HBM)] * 8,
        out_specs=pl.BlockSpec(memory_space=pltpu.VMEM),
        scratch_shapes=[
            vmem((ROWS, WIDTH), f32),
            vmem((HUBS, ROWS), bf16),
            pltpu.SMEM((HUB_OWN,), i32),
            vmem((SLOTS, ROWS), i32),
            vmem((1, ROWS), i32),
            vmem((16, SENT), i32),
            vmem((WIDTH, WIDTH), f32),
            vmem((1, WIDTH), f32),
            vmem((ROWS, WIDTH), bf16),
            vmem((ROWS, WIDTH), f32),
            vmem((ROWS, WIDTH), bf16),
            vmem((ROWS, WIDTH), bf16),
            vmem((16, SENT), i32),
            vmem((4 * SENT, ROWS), bf16),
            vmem((16, SENT, WIDTH), f32),
            vmem((16, SENT, WIDTH), f32),
            vmem((NC, HUBS, 128), f32),
            vmem((HUBS, 128), f32),
            vmem((NXL, NZ, 64, 128), f32),
            vmem((NZ - 1, NXL, 64, 128), f32),
            vmem((NXL, 8, 8, 128), f32),
            vmem((16, 8, 128), f32),
            vmem((2, ROWS, SLOTS), i32),
            vmem((ROWS, 8), f32),
            vmem((HUB_OWN, ROWS, WIDTH), f32),
            vmem((4, ROWS, 256), bf16),
            vmem((16, ROWS, SENT), bf16),
            vmem((ROWS, WIDTH), f32),
            vmem((WIDTH, WIDTH), bf16),
            vmem((WIDTH, WIDTH), bf16),
            dma((8,)), dma((16,)), dma((16,)), dma((2,)),
            dma((3,)), dma((3,)), dma((16,)), dma((16,)),
        ],
        compiler_params=pltpu.CompilerParams(
            collective_id=0, has_side_effects=True, vmem_limit_bytes=40 * 1024 * 1024
        ),
    )(
        *(
            pltpu.with_memory_space_constraint(array, pltpu.HBM)
            for array in (
                features, hub_block, hub_slot, neighbours.T, counts.reshape(1, -1), halo_send,
                weight, bias.reshape(1, -1),
            )
        )
    )


def solution(mesh):
    in_specs = (
        P(("grp", "loc"), None),
        P(None, ("grp", "loc")),
        P(("grp", "loc")),
        P(("grp", "loc"), None),
        P(("grp", "loc")),
        P(("grp", "loc"), None),
        P(),
        P(),
    )
    out_specs = P(("grp", "loc"), None)
    return jax.shard_map(
        on_device, mesh=mesh, in_specs=in_specs, out_specs=out_specs, check_vma=False
    )
```

time: 39.9 us -> 35.6 us (0.89)
  Pallas kernels: 38.8 us -> 34.5 us
    pallas_call x1, Pallas kernels: 38.8 us -> 34.5 us  [on_device(): pl.pallas_call(kernel, out_shape=jax.ShapeDtypeStruct((ROWS, WIDTH), f32)...]
where the time goes in v3:
time: 35.6 us; the launch traced here: 35.5 us
  Pallas kernels  34.5 us (97%)
  local copies, waits for them, and re-layouts  0.97 us (3%)
    pallas_call x1, Pallas kernels, on_device(): pl.pallas_call(kernel, out_shape=jax.ShapeDtypeStruct((ROWS, WIDTH), f32)...  34.5 us
    unnamed x1, local copies, waits for them, and re-layouts  0.97 us

profile of v3, /device:TPU:1, one launch (start us, length us, event | category | flops | bytes accessed | tf_op | source)
XLA Modules:
  0.0 35.5 jit_solution(9718315671789688898)
XLA Ops:
  0.0 34.5 %shard_map.82 = f32[1024,256]{1,0:T(8,128)S(1)} custom-call(f32[1024,256]{1,0:T(8,128)} %feat_hbm.1, bf16[512,1024]{1,0:T(8,128)(2,1)} %hub_hbm.1, s32[4]{0:T(128)} %slot_hbm.1, s32[16,1024]{1,0:T(8,128)} %bitcast.3, s32[1,1024]{1,0:T(1,128)} %bitcast.4, s32[16,128]{1,0:T(8,128)} %halo_hbm.1, f32[256,256]{1,0:T(8,128)} %weight_hbm.1, f32[1,256]{1,0:T(1,128)} %bitcast.5), custom_call_target="tpu_custom_call" | custom-call | tf_op jit(solution)/shard_map/pallas_call | solution.py:325
  34.5 1.0 %copy.10 = f32[1024,256]{1,0:T(8,128)} copy(f32[1024,256]{1,0:T(8,128)S(1)} %shard_map.82) | data formatting | bytes 2097152

commit v4 on v3

v4 whole, which is shorter than its diff:
```python
import jax
import jax.numpy as jnp
from jax import lax
from jax.experimental import pallas as pl
from jax.experimental.pallas import tpu as pltpu
from jax.sharding import PartitionSpec as P

MESH = pl.DeviceIdType.MESH
NY, NXH, NC, NXL, NZ = 4, 2, 2, 2, 4
ROWS, WIDTH, SLOTS, SENT = 1024, 256, 16, 128
HUBS, HUB_OWN = 512, 4
FIELD_ROWS, FIELDS, FIELD_BITS = 512, 6, 5

PLAN = (
    (((2, 1, 0), ), ()),
    (((1, 0, 0), (2, 1, 1), (3, 0, 0), ), ()),
    (((1, 1, 0), (2, 0, 0), (3, 1, 0), (2, 0, 1), (1, 0, 1), (3, 0, 1), (0, 0, 1), (0, 0, 0), ), ()),
    (((1, 1, 1), (3, 1, 1), ), ()),
    ((), ((2, 1, 0), )),
    ((), ((2, 1, 1), )),
    ((), ()),
    (((0, 1, 0), (0, 1, 1), ), ()),
    ((), ((1, 1, 0), )),
)
TAKE_ORDER = (
    ("take", (0, 0, 0)), ("take", (0, 0, 1)), ("forward", (3, 1, 0)),
    ("take", (1, 0, 0)), ("take", (3, 0, 0)), ("take", (2, 0, 0)),
    ("forward", (1, 1, 1)), ("take", (2, 0, 1)), ("take", (1, 0, 1)),
    ("take", (3, 0, 1)), ("take", (2, 1, 0)), ("forward", (3, 1, 1)),
    ("take", (2, 1, 1)), ("take", (1, 1, 0)), ("hub", (0, 0, 0)),
    ("take", (0, 1, 0)), ("take", (3, 1, 0)), ("last", (1, 1, 1)),
    ("last", (3, 1, 1)), ("last", (0, 1, 1)),
)


ORDER = tuple(step for sends, _ in PLAN for step in sends)
RELAYED = tuple(step for step in ORDER if step[0] != 0 and step[1] != 0)


def split2(value):
    high = value.astype(jnp.bfloat16)
    low = (value - high.astype(jnp.float32)).astype(jnp.bfloat16)
    return high, low


def mm(left, right):
    return jnp.dot(left, right, preferred_element_type=jnp.float32)


def scope(name):
    return jax.named_scope(name)


def kernel(
    feat_hbm, hub_hbm, slot_hbm, nbr_hbm, cnt_hbm, halo_hbm, weight_hbm, bias_hbm,
    out_ref,
    feat, hub, slot, nbr, cnt, halo, weight, bias,
    fhi, base, table, ghi, glo, stage, recv, relay,
    part, part_in, pair_sum, z_in, z_sum, plane_in,
    marks, recip, hub_mark, links_own, links_far, total, w_hi, w_lo,
    in_sem, halo_send, halo_recv, relay_send, relay_recv, a_sem, b_send, b_recv, c_send, c_recv, others_in,
):
    g, l = lax.axis_index("grp"), lax.axis_index("loc")
    y, xh, c = l // 4, (l // 2) % 2, l % 2
    xl, z = g // 4, g % 4
    x = xh * 2 + xl

    def loc_of(dy, dx, dc):
        return ((y + dy + 2 * c * dy) % NY) * 4 + ((xh + dx) % NXH) * 2 + (c + dc) % NC

    def loc_from(dy, dx, dc):
        source = (c + dc) % NC
        return ((y - dy - 2 * source * dy + 3 * NY) % NY) * 4 + ((xh + dx) % NXH) * 2 + source

    def plane_of(dx, dy):
        tx, ty = (x + dx) % 4, (y + dy) % NY
        return (tx % 2) * 4 + z, ty * 4 + (tx // 2) * 2 + c

    quarter = [pl.ds(start, 256) for start in range(0, ROWS, 256)]
    loads = []
    for number, (source, target) in enumerate((
        *((feat_hbm.at[q], feat.at[q]) for q in quarter), (weight_hbm, weight), (halo_hbm, halo),
        (hub_hbm, hub), (nbr_hbm, nbr), (cnt_hbm, cnt), (bias_hbm, bias), (slot_hbm, slot),
    )):
        copy = pltpu.make_async_copy(source, target, in_sem.at[number])
        copy.start()
        loads.append(copy)

    def signal(semaphore, where):
        pl.semaphore_signal(semaphore, inc=1, device_id=where, device_id_type=MESH)

    barrier = pltpu.get_barrier_semaphore()
    beside = (plane_of(1, 0), plane_of(3, 0))
    greeted = [(g, loc_of(*step)) for step in ORDER if step != (0, 0, 0)]
    greeted += beside
    for where in greeted:
        signal(barrier, where)
    ring = [(z + dz) % NZ for dz in range(1, NZ)]
    for to in ring:

        @pl.when((z != 0) & (to != 0))
        def _():
            signal(barrier, (xl * 4 + to, l))

    with scope("inputs"):
        loads[4].wait()
        w_hi[...], w_lo[...] = split2(weight[...])
        for copy in loads[:4]:
            copy.wait()

    def weighed(value):
        high, low = split2(value)
        return high, mm(high, w_hi[...]) + mm(low, w_hi[...]) + mm(high, w_lo[...])

    with scope("fw"):
        for start in range(0, ROWS, 256):
            rows = slice(start, start + 256)
            fhi[rows, :], value = weighed(feat[rows, :])
            for half in range(2):
                table[rows, half, :] = value[:, half * 128 : (half + 1) * 128]
        loads[5].wait()

    halo_copies, relay_copies, sent = {}, {}, []

    def gather(number):
        step = ORDER[number]
        peer = loc_of(*step)
        target = recv if step == (0, 0, 0) else stage
        for row in range(SENT):
            target[number, row] = table[halo[peer, row]]

    def start_copy(source, target, send_sem, recv_sem, where):
        copy = pltpu.make_async_remote_copy(
            src_ref=source, dst_ref=target, send_sem=send_sem, recv_sem=recv_sem,
            device_id=(g, where), device_id_type=MESH,
        )
        copy.start()
        sent.append(copy)
        return copy

    def send(step):
        number = ORDER.index(step)
        if step in RELAYED:
            at = RELAYED.index(step)
            relay_copies[step] = start_copy(
                stage.at[number], relay.at[at], halo_send.at[number], relay_recv.at[at],
                loc_of(0, 1, 0),
            )
        elif step != (0, 0, 0):
            halo_copies[step] = start_copy(
                stage.at[number], recv.at[number], halo_send.at[number], halo_recv.at[number],
                loc_of(*step),
            )

    def forward(step):
        number, at = ORDER.index(step), RELAYED.index(step)
        with scope(f"relay{step[0]}{step[2]}"):
            relay_copies[step].wait_recv()
        halo_copies[step] = start_copy(
            relay.at[at], recv.at[number], relay_send.at[at], halo_recv.at[number],
            loc_of(step[0], 0, step[2]),
        )

    def exchange(stage_number):
        for step in PLAN[stage_number][0]:
            if stage_number < 3 and step != ORDER[0]:
                gather(ORDER.index(step))
            send(step)
        for step in PLAN[stage_number][1]:
            forward(step)

    with scope("gather0"):
        gather(0)
    with scope("barrier"):
        pl.semaphore_wait(barrier, len(greeted) + jnp.where(z == 0, 0, NZ - 1))
    exchange(0)

    for to in ring:

        @pl.when((z == 0) | (to == 0))
        def _():
            signal(barrier, (xl * 4 + to, l))

    for number, where in enumerate(beside):
        signal(others_in.at[number], where)

    with scope("gather1"):
        exchange(1)

    with scope("hubpart"):
        loads[6].wait()
        upper = lax.broadcasted_iota(jnp.int32, (128, 128), 0) % 8 < 4
        for start in range(0, HUBS, 128):
            rows = mm(hub[start : start + 128, :], fhi[...])
            left, right = rows[:, :128], rows[:, 128:]
            part[0, start : start + 128, :] = jnp.where(upper, left, pltpu.roll(right, 4, 0))
            part[1, start : start + 128, :] = jnp.where(upper, pltpu.roll(left, 124, 0), right)
        pair_copy = pltpu.make_async_remote_copy(
            src_ref=part.at[1 - c],
            dst_ref=part_in,
            send_sem=a_sem.at[0],
            recv_sem=a_sem.at[1],
            device_id=(g, loc_of(0, 0, 1)),
            device_id_type=MESH,
        )
        pair_copy.start()

    with scope("gather2"):
        exchange(2)
        for number in range(sum(len(sends) for sends, _ in PLAN[:3]), len(ORDER)):
            gather(number)

    with scope("a_to_b"):
        pair_copy.wait_recv()
        pair_sum[...] = (part[pl.ds(c, 1)][0] + part_in[...]).reshape(NXL, NZ, 64, 128)
        z_copies = []

        @pl.when(z == 0)
        def _():
            pl.semaphore_wait(barrier, NZ - 1)

        for dz in range(1, NZ):
            to = (z + dz) % NZ
            copy = pltpu.make_async_remote_copy(
                src_ref=pair_sum.at[:, to],
                dst_ref=z_in.at[dz - 1],
                send_sem=b_send.at[dz - 1],
                recv_sem=b_recv.at[dz - 1],
                device_id=(xl * 4 + to, l),
                device_id_type=MESH,
            )
            copy.start()
            z_copies.append(copy)


    with scope("marks"):
        loads[7].wait()
        loads[8].wait()
        slots, used = nbr[...], cnt[...]
        active = lax.broadcasted_iota(jnp.int32, (SLOTS, ROWS), 0) < used
        place = slots & (FIELD_ROWS - 1)
        one = jnp.where(active, jnp.left_shift(1, (slots >> 9) * FIELD_BITS), 0)
        inverse = jnp.broadcast_to(1.0 / used.astype(jnp.float32), (8, ROWS))
        for start in range(0, ROWS, 128):
            rows = slice(start, start + 128)
            marks[0, rows, :] = place[:, rows].T
            marks[1, rows, :] = one[:, rows].T
            recip[rows, :] = inverse[:, rows].T

    pool_lane = lax.broadcasted_iota(jnp.int32, (32, FIELD_ROWS), 1)

    def build(block, carry):
        rows = pl.ds(pl.multiple_of(block * 32, 32), 32)
        row_place, row_one = marks[0, rows, :], marks[1, rows, :]
        packed = jnp.zeros((32, FIELD_ROWS), jnp.int32)
        for k in range(SLOTS):
            packed = packed + jnp.where(
                row_place[:, k : k + 1] == pool_lane, row_one[:, k : k + 1], 0
            )
        for field in range(FIELDS):
            number = (packed >> (field * FIELD_BITS)) & (2**FIELD_BITS - 1)
            number = number.astype(jnp.float32).astype(jnp.bfloat16)
            if field < 2:
                links_own[2 * field, rows, :] = number[:, :256]
                links_own[2 * field + 1, rows, :] = number[:, 256:]
            else:
                for peer in range(4):
                    links = number[:, peer * SENT : (peer + 1) * SENT]
                    for half in range(2):
                        lanes = slice(half * SENT, (half + 1) * SENT)
                        links_far[(field - 2) * 4 + peer, rows, lanes] = links
        return carry

    exchange(3)
    with scope("build1"):
        lax.fori_loop(0, 8, build, 0)
    exchange(4)
    with scope("build2"):
        lax.fori_loop(8, 16, build, 0)
    exchange(5)
    with scope("build3"):
        lax.fori_loop(16, 24, build, 0)
    exchange(6)
    with scope("b_to_c"):
        for copy in z_copies:
            copy.wait_recv()
        for half in range(NXL):
            value = pair_sum[half, pl.ds(z, 1)][0]
            for dz in range(NZ - 1):
                value = value + z_in[dz, half]
            z_sum[half] = value.reshape(8, 8, 128)
        plane_copies = []
        for number in (0, 1):
            pl.semaphore_wait(others_in.at[number], 1)
        for dx in range(4):
            for dy in range(NY):
                if (dx, dy) == (0, 0):
                    continue
                tx, ty = (x + dx) % 4, (y + dy) % NY
                copy = pltpu.make_async_remote_copy(
                    src_ref=z_sum.at[tx % 2, ty * 2 + tx // 2],
                    dst_ref=plane_in.at[dx * 4 + dy],
                    send_sem=c_send.at[dx * 4 + dy],
                    recv_sem=c_recv.at[dx * 4 + dy],
                    device_id=plane_of(dx, dy),
                    device_id_type=MESH,
                )
                copy.start()
                plane_copies.append(copy)

    exchange(7)
    with scope("build4"):
        lax.fori_loop(24, 32, build, 0)
    exchange(8)

    with scope("hub_mark"):
        loads[9].wait()
        loads[10].wait()
        vertex = lax.broadcasted_iota(jnp.int32, (ROWS, 128), 0)
        lane = lax.broadcasted_iota(jnp.int32, (ROWS, 128), 1)
        mark = jnp.zeros((ROWS, 128), jnp.float32)
        for r in range(HUB_OWN):
            mark = jnp.where((vertex == slot[r]) & ((lane == r) | (lane == 4 + r)), 1.0, mark)
        hub_mark[...] = mark.astype(jnp.bfloat16)
        for start in range(0, ROWS, 256):
            rows = slice(start, start + 256)
            halves = [table[rows, half, :] for half in range(2)]
            value = jnp.concatenate(halves, axis=1)
            base[rows, :] = value + bias[...]
            ghi[rows, :], glo[rows, :] = split2(value)

    with scope("own"):
        for number in range(4):
            rows = slice(number * 256, (number + 1) * 256)
            value = mm(links_own[number], ghi[rows, :]) + mm(links_own[number], glo[rows, :])
            total[...] = value if number == 0 else total[...] + value

    def far(step):
        number = ORDER.index(step)
        dy, dx, dc = step
        if step != (0, 0, 0):
            with scope(f"wait{dy}{dx}{dc}"):
                halo_copies[step].wait_recv()
        peer = loc_from(dy, dx, dc)
        halves = [recv[number, :, half, :] for half in range(2)]
        high, low = split2(jnp.concatenate(halves, axis=1))
        return peer, jnp.concatenate([high, low], axis=0)

    def linked(peer, rows):
        return links_far[pl.ds(peer, 1), rows, :][0]

    def hub_rows():
        with scope("wait_c"):
            for copy in plane_copies:
                copy.wait_recv()
        with scope("hub_rows"):
            hub_tile = z_sum[pl.ds(xl, 1), pl.ds(y * 2 + xh, 1)][0, 0]
            for source in range(1, 16):
                hub_tile = hub_tile + plane_in[source]
            hub_own = weighed(jnp.concatenate([hub_tile, pltpu.roll(hub_tile, 4, 0)], axis=1))[1]
            upper = lax.broadcasted_iota(jnp.int32, (8, WIDTH), 0) < HUB_OWN
            high = hub_own.astype(jnp.bfloat16).astype(jnp.float32)
            both = jnp.where(upper, high, pltpu.roll(hub_own - high, 4, 0))
            hub_values = jnp.concatenate([both, jnp.zeros((120, WIDTH), jnp.float32)], axis=0)
            hub_values = hub_values.astype(jnp.bfloat16)
            base[...] += mm(hub_mark[...], hub_values)

    for kind, step in TAKE_ORDER:
        if kind == "hub":
            hub_rows()
        elif kind == "forward":
            forward(step)
        elif kind == "take":
            peer, values = far(step)
            with scope("take"):
                total[...] += mm(linked(peer, slice(None)), values)

    with scope("combine"):
        base[...] += total[...] * recip[:, 0:1]
    last = [far(step) for kind, step in TAKE_ORDER if kind == "last"]
    with scope("final"):
        for start in range(0, ROWS, 256):
            rows = slice(start, start + 256)
            value = sum(mm(linked(peer, rows), values) for peer, values in last)
            out_ref[rows, :] = jnp.maximum(base[rows, :] + value * recip[rows, 0:1], 0.0)

    with scope("wait_send"):
        for copy in sent:
            copy.wait_send()
        pair_copy.wait_send()
        for copy in z_copies + plane_copies:
            copy.wait_send()


def on_device(features, hub_block, hub_slot, neighbours, counts, halo_send, weight, bias):
    f32, bf16, i32 = jnp.float32, jnp.bfloat16, jnp.int32
    vmem, dma = pltpu.VMEM, pltpu.SemaphoreType.DMA
    return pl.pallas_call(
        kernel,
        out_shape=jax.ShapeDtypeStruct((ROWS, WIDTH), f32),
        in_specs=[pl.BlockSpec(memory_space=pltpu.HBM)] * 8,
        out_specs=pl.BlockSpec(memory_space=pltpu.VMEM),
        scratch_shapes=[
            vmem((ROWS, WIDTH), f32),
            vmem((HUBS, ROWS), bf16),
            pltpu.SMEM((HUB_OWN,), i32),
            vmem((SLOTS, ROWS), i32),
            vmem((1, ROWS), i32),
            pltpu.SMEM((16, SENT), i32),
            vmem((WIDTH, WIDTH), f32),
            vmem((1, WIDTH), f32),
            vmem((ROWS, WIDTH), bf16),
            vmem((ROWS, WIDTH), f32),
            vmem((ROWS, 2, 128), f32),
            vmem((ROWS, WIDTH), bf16),
            vmem((ROWS, WIDTH), bf16),
            vmem((16, SENT, 2, 128), f32),
            vmem((16, SENT, 2, 128), f32),
            vmem((6, SENT, 2, 128), f32),
            vmem((NC, HUBS, 128), f32),
            vmem((HUBS, 128), f32),
            vmem((NXL, NZ, 64, 128), f32),
            vmem((NZ - 1, NXL, 64, 128), f32),
            vmem((NXL, 8, 8, 128), f32),
            vmem((16, 8, 128), f32),
            vmem((2, ROWS, SLOTS), i32),
            vmem((ROWS, 8), f32),
            vmem((ROWS, 128), bf16),
            vmem((4, ROWS, 256), bf16),
            vmem((16, ROWS, 2 * SENT), bf16),
            vmem((ROWS, WIDTH), f32),
            vmem((WIDTH, WIDTH), bf16),
            vmem((WIDTH, WIDTH), bf16),
            dma((11,)), dma((16,)), dma((16,)), dma((6,)), dma((6,)), dma((2,)),
            dma((3,)), dma((3,)), dma((16,)), dma((16,)), pltpu.SemaphoreType.REGULAR((2,)),
        ],
        compiler_params=pltpu.CompilerParams(
            collective_id=0, has_side_effects=True, vmem_limit_bytes=40 * 1024 * 1024
        ),
    )(
        *(
            pltpu.with_memory_space_constraint(array, pltpu.HBM)
            for array in (
                features, hub_block, hub_slot, neighbours.T, counts.reshape(1, -1), halo_send,
                weight, bias.reshape(1, -1),
            )
        )
    )


def solution(mesh):
    in_specs = (
        P(("grp", "loc"), None),
        P(None, ("grp", "loc")),
        P(("grp", "loc")),
        P(("grp", "loc"), None),
        P(("grp", "loc")),
        P(("grp", "loc"), None),
        P(),
        P(),
    )
    out_specs = P(("grp", "loc"), None)
    return jax.shard_map(
        on_device, mesh=mesh, in_specs=in_specs, out_specs=out_specs, check_vma=False
    )
```

time: 35.6 us -> 35.8 us (level)
  no operation moved by 1% of the time
where the time goes in v4:
time: 35.8 us; the launch traced here: 35.7 us
  Pallas kernels  34.7 us (97%)
  local copies, waits for them, and re-layouts  0.97 us (3%)
    pallas_call x1, Pallas kernels, on_device(): pl.pallas_call(kernel, out_shape=jax.ShapeDtypeStruct((ROWS, WIDTH), f32)...  34.7 us
    unnamed x1, local copies, waits for them, and re-layouts  0.97 us

profile of v4, /device:TPU:1, one launch (start us, length us, event | category | flops | bytes accessed | tf_op | source)
XLA Modules:
  0.0 35.7 jit_solution(4600210940512313373)
XLA Ops:
  0.0 34.7 %shard_map.82 = f32[1024,256]{1,0:T(8,128)S(1)} custom-call(f32[1024,256]{1,0:T(8,128)} %feat_hbm.1, bf16[512,1024]{1,0:T(8,128)(2,1)} %hub_hbm.1, s32[4]{0:T(128)} %slot_hbm.1, s32[16,1024]{1,0:T(8,128)} %bitcast.3, s32[1,1024]{1,0:T(1,128)} %bitcast.4, s32[16,128]{1,0:T(8,128)} %halo_hbm.1, f32[256,256]{1,0:T(8,128)} %weight_hbm.1, f32[1,256]{1,0:T(1,128)} %bitcast.5), custom_call_target="tpu_custom_call" | custom-call | tf_op jit(solution)/shard_map/pallas_call | solution.py:398
  34.7 1.0 %copy.10 = f32[1024,256]{1,0:T(8,128)} copy(f32[1024,256]{1,0:T(8,128)S(1)} %shard_map.82) | data formatting | bytes 2097152

commit v5 on v4

--- a/solution.py
+++ b/solution.py
@@ -90,9 +90,9 @@
         pl.semaphore_signal(semaphore, inc=1, device_id=where, device_id_type=MESH)
 
     barrier = pltpu.get_barrier_semaphore()
-    beside = (plane_of(1, 0), plane_of(3, 0))
-    greeted = [(g, loc_of(*step)) for step in ORDER if step != (0, 0, 0)]
-    greeted += beside
+    beside = (plane_of(1, 0), plane_of(3, 0), plane_of(2, 0))
+    greeted = [(g, loc_of(*step)) for step in ORDER if step != (0, 0, 0) and step not in RELAYED]
+    greeted += beside[:2]
     for where in greeted:
         signal(barrier, where)
     ring = [(z + dz) % NZ for dz in range(1, NZ)]
@@ -117,17 +117,19 @@
             rows = slice(start, start + 256)
             fhi[rows, :], value = weighed(feat[rows, :])
             for half in range(2):
-                table[rows, half, :] = value[:, half * 128 : (half + 1) * 128]
+                table[pl.ds(2 * start + half, 256, stride=2), :] = value[:, half * 128 : (half + 1) * 128]
         loads[5].wait()
 
     halo_copies, relay_copies, sent = {}, {}, []
+
+    by_row = table.reshape(ROWS, 2, 128)
 
     def gather(number):
         step = ORDER[number]
         peer = loc_of(*step)
         target = recv if step == (0, 0, 0) else stage
         for row in range(SENT):
-            target[number, row] = table[halo[peer, row]]
+            target[number, row] = by_row[halo[peer, row]]
 
     def start_copy(source, target, send_sem, recv_sem, where):
         copy = pltpu.make_async_remote_copy(
@@ -290,7 +292,7 @@
                 value = value + z_in[dz, half]
             z_sum[half] = value.reshape(8, 8, 128)
         plane_copies = []
-        for number in (0, 1):
+        for number in range(3):
             pl.semaphore_wait(others_in.at[number], 1)
         for dx in range(4):
             for dy in range(NY):
@@ -324,7 +326,7 @@
         hub_mark[...] = mark.astype(jnp.bfloat16)
         for start in range(0, ROWS, 256):
             rows = slice(start, start + 256)
-            halves = [table[rows, half, :] for half in range(2)]
+            halves = [table[pl.ds(2 * start + half, 256, stride=2), :] for half in range(2)]
             value = jnp.concatenate(halves, axis=1)
             base[rows, :] = value + bias[...]
             ghi[rows, :], glo[rows, :] = split2(value)
@@ -411,7 +413,7 @@
             vmem((1, WIDTH), f32),
             vmem((ROWS, WIDTH), bf16),
             vmem((ROWS, WIDTH), f32),
-            vmem((ROWS, 2, 128), f32),
+            vmem((2 * ROWS, 128), f32),
             vmem((ROWS, WIDTH), bf16),
             vmem((ROWS, WIDTH), bf16),
             vmem((16, SENT, 2, 128), f32),
@@ -432,7 +434,7 @@
             vmem((WIDTH, WIDTH), bf16),
             vmem((WIDTH, WIDTH), bf16),
             dma((11,)), dma((16,)), dma((16,)), dma((6,)), dma((6,)), dma((2,)),
-            dma((3,)), dma((3,)), dma((16,)), dma((16,)), pltpu.SemaphoreType.REGULAR((2,)),
+            dma((3,)), dma((3,)), dma((16,)), dma((16,)), pltpu.SemaphoreType.REGULAR((3,)),
         ],
         compiler_params=pltpu.CompilerParams(
             collective_id=0, has_side_effects=True, vmem_limit_bytes=40 * 1024 * 1024

time: 35.8 us -> 35.1 us (0.980)
  Pallas kernels: 34.7 us -> 33.9 us
    pallas_call x1, Pallas kernels: 34.7 us -> 33.9 us  [on_device(): pl.pallas_call(kernel, out_shape=jax.ShapeDtypeStruct((ROWS, WIDTH), f32)...]
where the time goes in v5:
time: 35.1 us; the launch traced here: 34.9 us
  Pallas kernels  33.9 us (97%)
  local copies, waits for them, and re-layouts  0.97 us (3%)
    pallas_call x1, Pallas kernels, on_device(): pl.pallas_call(kernel, out_shape=jax.ShapeDtypeStruct((ROWS, WIDTH), f32)...  33.9 us
    unnamed x1, local copies, waits for them, and re-layouts  0.97 us

profile of v5, /device:TPU:1, one launch (start us, length us, event | category | flops | bytes accessed | tf_op | source)
XLA Modules:
  0.0 34.9 jit_solution(1997616250286745482)
XLA Ops:
  0.0 33.9 %shard_map.82 = f32[1024,256]{1,0:T(8,128)S(1)} custom-call(f32[1024,256]{1,0:T(8,128)} %feat_hbm.1, bf16[512,1024]{1,0:T(8,128)(2,1)} %hub_hbm.1, s32[4]{0:T(128)} %slot_hbm.1, s32[16,1024]{1,0:T(8,128)} %bitcast.3, s32[1,1024]{1,0:T(1,128)} %bitcast.4, s32[16,128]{1,0:T(8,128)} %halo_hbm.1, f32[256,256]{1,0:T(8,128)} %weight_hbm.1, f32[1,256]{1,0:T(1,128)} %bitcast.5), custom_call_target="tpu_custom_call" | custom-call | tf_op jit(solution)/shard_map/pallas_call | solution.py:400
  34.0 1.0 %copy.10 = f32[1024,256]{1,0:T(8,128)} copy(f32[1024,256]{1,0:T(8,128)S(1)} %shard_map.82) | data formatting | bytes 2097152

commit v6 on v5

--- a/solution.py
+++ b/solution.py
@@ -28,8 +28,8 @@
     ("forward", (1, 1, 1)), ("take", (2, 0, 1)), ("take", (1, 0, 1)),
     ("take", (3, 0, 1)), ("take", (2, 1, 0)), ("forward", (3, 1, 1)),
     ("take", (2, 1, 1)), ("take", (1, 1, 0)), ("hub", (0, 0, 0)),
-    ("take", (0, 1, 0)), ("take", (3, 1, 0)), ("last", (1, 1, 1)),
-    ("last", (3, 1, 1)), ("last", (0, 1, 1)),
+    ("take", (0, 1, 0)), ("take", (3, 1, 0)), ("take", (0, 1, 1)),
+    ("last", (1, 1, 1)), ("last", (3, 1, 1)),
 )
 
 

time: 35.1 us -> 34.7 us (0.989)
  no operation moved by 1% of the time
where the time goes in v6:
time: 34.7 us; the launch traced here: 34.6 us
  Pallas kernels  33.6 us (97%)
  local copies, waits for them, and re-layouts  0.97 us (3%)
    pallas_call x1, Pallas kernels, on_device(): pl.pallas_call(kernel, out_shape=jax.ShapeDtypeStruct((ROWS, WIDTH), f32)...  33.6 us
    unnamed x1, local copies, waits for them, and re-layouts  0.97 us

profile of v6, /device:TPU:1, one launch (start us, length us, event | category | flops | bytes accessed | tf_op | source)
XLA Modules:
  0.0 34.6 jit_solution(11673456831109722336)
XLA Ops:
  0.0 33.6 %shard_map.82 = f32[1024,256]{1,0:T(8,128)S(1)} custom-call(f32[1024,256]{1,0:T(8,128)} %feat_hbm.1, bf16[512,1024]{1,0:T(8,128)(2,1)} %hub_hbm.1, s32[4]{0:T(128)} %slot_hbm.1, s32[16,1024]{1,0:T(8,128)} %bitcast.3, s32[1,1024]{1,0:T(1,128)} %bitcast.4, s32[16,128]{1,0:T(8,128)} %halo_hbm.1, f32[256,256]{1,0:T(8,128)} %weight_hbm.1, f32[1,256]{1,0:T(1,128)} %bitcast.5), custom_call_target="tpu_custom_call" | custom-call | tf_op jit(solution)/shard_map/pallas_call | solution.py:400
  33.6 1.0 %copy.10 = f32[1024,256]{1,0:T(8,128)} copy(f32[1024,256]{1,0:T(8,128)S(1)} %shard_map.82) | data formatting | bytes 2097152

commit v7 on v6

--- a/solution.py
+++ b/solution.py
@@ -34,6 +34,7 @@
 
 
 ORDER = tuple(step for sends, _ in PLAN for step in sends)
+LAST = sum(kind == "last" for kind, _ in TAKE_ORDER)
 RELAYED = tuple(step for step in ORDER if step[0] != 0 and step[1] != 0)
 
 
@@ -53,11 +54,11 @@
 
 def kernel(
     feat_hbm, hub_hbm, slot_hbm, nbr_hbm, cnt_hbm, halo_hbm, weight_hbm, bias_hbm,
-    out_ref,
+    base, recip, last_links, last_values,
     feat, hub, slot, nbr, cnt, halo, weight, bias,
-    fhi, base, table, ghi, glo, stage, recv, relay,
+    fhi, table, ghi, glo, stage, recv, relay,
     part, part_in, pair_sum, z_in, z_sum, plane_in,
-    marks, recip, hub_mark, links_own, links_far, total, w_hi, w_lo,
+    marks, hub_mark, links_own, links_far, total, w_hi, w_lo,
     in_sem, halo_send, halo_recv, relay_send, relay_recv, a_sem, b_send, b_recv, c_send, c_recv, others_in,
 ):
     g, l = lax.axis_index("grp"), lax.axis_index("loc")
@@ -379,12 +380,11 @@
 
     with scope("combine"):
         base[...] += total[...] * recip[:, 0:1]
-    last = [far(step) for kind, step in TAKE_ORDER if kind == "last"]
-    with scope("final"):
-        for start in range(0, ROWS, 256):
-            rows = slice(start, start + 256)
-            value = sum(mm(linked(peer, rows), values) for peer, values in last)
-            out_ref[rows, :] = jnp.maximum(base[rows, :] + value * recip[rows, 0:1], 0.0)
+        last = [step for kind, step in TAKE_ORDER if kind == "last"]
+        for number, step in enumerate(last):
+            last_links[number] = linked(loc_from(*step), slice(None))
+    for number, step in enumerate(last):
+        last_values[number] = far(step)[1]
 
     with scope("wait_send"):
         for copy in sent:
@@ -394,14 +394,33 @@
             copy.wait_send()
 
 
+def finish(base, recip, last_links, last_values, out_hbm, out, out_sem):
+    copies = []
+    for start in range(0, ROWS, 256):
+        rows = slice(start, start + 256)
+        value = sum(mm(last_links[number, rows, :], last_values[number]) for number in range(LAST))
+        out[rows, :] = jnp.maximum(base[rows, :] + value * recip[rows, 0:1], 0.0)
+        piece = pl.ds(start, 256)
+        copy = pltpu.make_async_copy(out.at[piece], out_hbm.at[piece], out_sem.at[start // 256])
+        copy.start()
+        copies.append(copy)
+    for copy in copies:
+        copy.wait()
+
+
 def on_device(features, hub_block, hub_slot, neighbours, counts, halo_send, weight, bias):
     f32, bf16, i32 = jnp.float32, jnp.bfloat16, jnp.int32
     vmem, dma = pltpu.VMEM, pltpu.SemaphoreType.DMA
-    return pl.pallas_call(
+    handed = pl.pallas_call(
         kernel,
-        out_shape=jax.ShapeDtypeStruct((ROWS, WIDTH), f32),
+        out_shape=(
+            jax.ShapeDtypeStruct((ROWS, WIDTH), f32),
+            jax.ShapeDtypeStruct((ROWS, 8), f32),
+            jax.ShapeDtypeStruct((LAST, ROWS, 2 * SENT), bf16),
+            jax.ShapeDtypeStruct((LAST, 2 * SENT, WIDTH), bf16),
+        ),
         in_specs=[pl.BlockSpec(memory_space=pltpu.HBM)] * 8,
-        out_specs=pl.BlockSpec(memory_space=pltpu.VMEM),
+        out_specs=(pl.BlockSpec(memory_space=pltpu.VMEM),) * 4,
         scratch_shapes=[
             vmem((ROWS, WIDTH), f32),
             vmem((HUBS, ROWS), bf16),
@@ -412,7 +431,6 @@
             vmem((WIDTH, WIDTH), f32),
             vmem((1, WIDTH), f32),
             vmem((ROWS, WIDTH), bf16),
-            vmem((ROWS, WIDTH), f32),
             vmem((2 * ROWS, 128), f32),
             vmem((ROWS, WIDTH), bf16),
             vmem((ROWS, WIDTH), bf16),
@@ -426,7 +444,6 @@
             vmem((NXL, 8, 8, 128), f32),
             vmem((16, 8, 128), f32),
             vmem((2, ROWS, SLOTS), i32),
-            vmem((ROWS, 8), f32),
             vmem((ROWS, 128), bf16),
             vmem((4, ROWS, 256), bf16),
             vmem((16, ROWS, 2 * SENT), bf16),
@@ -448,6 +465,14 @@
             )
         )
     )
+    return pl.pallas_call(
+        finish,
+        out_shape=jax.ShapeDtypeStruct((ROWS, WIDTH), f32),
+        in_specs=[pl.BlockSpec(memory_space=pltpu.VMEM)] * 4,
+        out_specs=pl.BlockSpec(memory_space=pl.ANY),
+        scratch_shapes=[vmem((ROWS, WIDTH), f32), dma((4,))],
+        compiler_params=pltpu.CompilerParams(vmem_limit_bytes=8 * 1024 * 1024),
+    )(*handed)
 
 
 def solution(mesh):

time: 34.7 us -> 34.4 us (level)
  local copies, waits for them, and re-layouts: 0.97 us -> 0 us
  Pallas kernels: 33.6 us -> 34.3 us
    unnamed x1 -> x0, local copies, waits for them, and re-layouts: 0.97 us -> none
    pallas_call x1 -> x2, Pallas kernels: 33.6 us -> 34.3 us  [the longest x1 33 us: on_device(): pl.pallas_call(kernel, out_shape=(jax.ShapeDtypeStruct((ROWS, WIDTH), f32...]
where the time goes in v7:
time: 34.4 us; the launch traced here: 34.3 us
  Pallas kernels  34.3 us (100%)
    pallas_call x1, Pallas kernels, on_device(): pl.pallas_call(kernel, out_shape=(jax.ShapeDtypeStruct((ROWS, WIDTH), f32...  33 us
    pallas_call x1, Pallas kernels, on_device(): pl.pallas_call(finish, out_shape=jax.ShapeDtypeStruct((ROWS, WIDTH), f32)...  1.31 us

profile of v7, /device:TPU:1, one launch (start us, length us, event | category | flops | bytes accessed | tf_op | source)
XLA Modules:
  0.0 34.3 jit_solution(15824267077598557283)
XLA Ops:
  0.0 33.0 %shard_map.82 = (f32[1024,256]{1,0:T(8,128)S(1)}, f32[1024,8]{1,0:T(8,128)S(1)}, bf16[2,1024,256]{2,1,0:T(8,128)(2,1)S(1)}, bf16[2,256,256]{2,1,0:T(8,128)(2,1)S(1)}) custom-call(f32[1024,256]{1,0:T(8,128)} %feat_hbm.1, bf16[512,1024]{1,0:T(8,128)(2,1)} %hub_hbm.1, s32[4]{0:T(128)} %slot_hbm.1, s32[16,1024]{1,0:T(8,128)} %bitcast.3, s32[1,1024]{1,0:T(1,128)} %bitcast.4, ...), custom_call_target="tpu_custom_call" | custom-call | tf_op jit(solution)/shard_map/pallas_call | solution.py:414
  33.0 1.3 %shard_map.83 = f32[1024,256]{1,0:T(8,128)} custom-call(f32[1024,256]{1,0:T(8,128)S(1)} %get-tuple-element.9.base, f32[1024,8]{1,0:T(8,128)S(1)} %get-tuple-element.10.recip, bf16[2,1024,256]{2,1,0:T(8,128)(2,1)S(1)} %get-tuple-element.11.last_links, bf16[2,256,256]{2,1,0:T(8,128)(2,1)S(1)} %get-tuple-element.12.last_values), custom_call_target="tpu_custom_call" | custom-call | tf_op jit(solution)/shard_map/pallas_call | solution.py:468

commit v8 on v7

--- a/solution.py
+++ b/solution.py
@@ -28,7 +28,7 @@
     ("forward", (1, 1, 1)), ("take", (2, 0, 1)), ("take", (1, 0, 1)),
     ("take", (3, 0, 1)), ("take", (2, 1, 0)), ("forward", (3, 1, 1)),
     ("take", (2, 1, 1)), ("take", (1, 1, 0)), ("hub", (0, 0, 0)),
-    ("take", (0, 1, 0)), ("take", (3, 1, 0)), ("take", (0, 1, 1)),
+    ("take", (0, 1, 0)), ("take", (3, 1, 0)), ("combine", (0, 0, 0)), ("take", (0, 1, 1)),
     ("last", (1, 1, 1)), ("last", (3, 1, 1)),
 )
 
@@ -368,21 +368,28 @@
             hub_values = hub_values.astype(jnp.bfloat16)
             base[...] += mm(hub_mark[...], hub_values)
 
+    last = [step for kind, step in TAKE_ORDER if kind == "last"]
+    combined = False
     for kind, step in TAKE_ORDER:
         if kind == "hub":
             hub_rows()
         elif kind == "forward":
             forward(step)
+        elif kind == "combine":
+            with scope("combine"):
+                base[...] += total[...] * recip[:, 0:1]
+                for number, later in enumerate(last):
+                    last_links[number] = linked(loc_from(*later), slice(None))
+            combined = True
         elif kind == "take":
             peer, values = far(step)
             with scope("take"):
-                total[...] += mm(linked(peer, slice(None)), values)
-
-    with scope("combine"):
-        base[...] += total[...] * recip[:, 0:1]
-        last = [step for kind, step in TAKE_ORDER if kind == "last"]
-        for number, step in enumerate(last):
-            last_links[number] = linked(loc_from(*step), slice(None))
+                value = mm(linked(peer, slice(None)), values)
+                if combined:
+                    base[...] += value * recip[:, 0:1]
+                else:
+                    total[...] += value
+
     for number, step in enumerate(last):
         last_values[number] = far(step)[1]
 

time: 34.4 us -> 34.4 us (level)
  no operation moved by 1% of the time
where the time goes in v8:
time: 34.4 us; the launch traced here: 34.3 us
  Pallas kernels  34.3 us (100%)
    pallas_call x1, Pallas kernels, on_device(): pl.pallas_call(kernel, out_shape=(jax.ShapeDtypeStruct((ROWS, WIDTH), f32...  32.9 us
    pallas_call x1, Pallas kernels, on_device(): pl.pallas_call(finish, out_shape=jax.ShapeDtypeStruct((ROWS, WIDTH), f32)...  1.32 us

profile of v8, /device:TPU:1, one launch (start us, length us, event | category | flops | bytes accessed | tf_op | source)
XLA Modules:
  0.0 34.3 jit_solution(9242842426996024309)
XLA Ops:
  0.0 32.9 %shard_map.82 = (f32[1024,256]{1,0:T(8,128)S(1)}, f32[1024,8]{1,0:T(8,128)S(1)}, bf16[2,1024,256]{2,1,0:T(8,128)(2,1)S(1)}, bf16[2,256,256]{2,1,0:T(8,128)(2,1)S(1)}) custom-call(f32[1024,256]{1,0:T(8,128)} %feat_hbm.1, bf16[512,1024]{1,0:T(8,128)(2,1)} %hub_hbm.1, s32[4]{0:T(128)} %slot_hbm.1, s32[16,1024]{1,0:T(8,128)} %bitcast.3, s32[1,1024]{1,0:T(1,128)} %bitcast.4, ...), custom_call_target="tpu_custom_call" | custom-call | tf_op jit(solution)/shard_map/pallas_call | solution.py:421
  33.0 1.3 %shard_map.83 = f32[1024,256]{1,0:T(8,128)} custom-call(f32[1024,256]{1,0:T(8,128)S(1)} %get-tuple-element.9.base, f32[1024,8]{1,0:T(8,128)S(1)} %get-tuple-element.10.recip, bf16[2,1024,256]{2,1,0:T(8,128)(2,1)S(1)} %get-tuple-element.11.last_links, bf16[2,256,256]{2,1,0:T(8,128)(2,1)S(1)} %get-tuple-element.12.last_values), custom_call_target="tpu_custom_call" | custom-call | tf_op jit(solution)/shard_map/pallas_call | solution.py:475

commit v9 on v8

--- a/solution.py
+++ b/solution.py
@@ -29,7 +29,7 @@
     ("take", (3, 0, 1)), ("take", (2, 1, 0)), ("forward", (3, 1, 1)),
     ("take", (2, 1, 1)), ("take", (1, 1, 0)), ("hub", (0, 0, 0)),
     ("take", (0, 1, 0)), ("take", (3, 1, 0)), ("combine", (0, 0, 0)), ("take", (0, 1, 1)),
-    ("last", (1, 1, 1)), ("last", (3, 1, 1)),
+    ("take", (3, 1, 1)), ("last", (1, 1, 1)),
 )
 
 

time: 34.4 us -> 34.7 us (level)
  no operation moved by 1% of the time
where the time goes in v9:
time: 34.7 us; the launch traced here: 34.5 us
  Pallas kernels  34.5 us (99%)
    pallas_call x1, Pallas kernels, on_device(): pl.pallas_call(kernel, out_shape=(jax.ShapeDtypeStruct((ROWS, WIDTH), f32...  33.3 us
    pallas_call x1, Pallas kernels, on_device(): pl.pallas_call(finish, out_shape=jax.ShapeDtypeStruct((ROWS, WIDTH), f32)...  1.24 us

profile of v9, /device:TPU:1, one launch (start us, length us, event | category | flops | bytes accessed | tf_op | source)
XLA Modules:
  0.0 34.5 jit_solution(6828667976819297091)
XLA Ops:
  0.0 33.3 %shard_map.82 = (f32[1024,256]{1,0:T(8,128)S(1)}, f32[1024,8]{1,0:T(8,128)S(1)}, bf16[1,1024,256]{2,1,0:T(8,128)(2,1)S(1)}, bf16[1,256,256]{2,1,0:T(8,128)(2,1)S(1)}) custom-call(f32[1024,256]{1,0:T(8,128)} %feat_hbm.1, bf16[512,1024]{1,0:T(8,128)(2,1)} %hub_hbm.1, s32[4]{0:T(128)} %slot_hbm.1, s32[16,1024]{1,0:T(8,128)} %bitcast.3, s32[1,1024]{1,0:T(1,128)} %bitcast.4, ...), custom_call_target="tpu_custom_call" | custom-call | tf_op jit(solution)/shard_map/pallas_call | solution.py:421
  33.3 1.2 %shard_map.83 = f32[1024,256]{1,0:T(8,128)} custom-call(f32[1024,256]{1,0:T(8,128)S(1)} %get-tuple-element.9.base, f32[1024,8]{1,0:T(8,128)S(1)} %get-tuple-element.10.recip, bf16[1,1024,256]{2,1,0:T(8,128)(2,1)S(1)} %get-tuple-element.11.last_links, bf16[1,256,256]{2,1,0:T(8,128)(2,1)S(1)} %get-tuple-element.12.last_values), custom_call_target="tpu_custom_call" | custom-call | tf_op jit(solution)/shard_map/pallas_call | solution.py:475
